TPU v7x, 32 devices: a whole 2x2x4 slice. The times are simulated.
32 devices in a mesh: grp: 4 (over y, x), dom: 8 (over z, core).
Axes of the slice: x: 2, y: 2, z: 4, core: 2. Of those that a mesh axis runs over, the one named last changes fastest.
Arguments:
- forcing: float32 [3, 2048, 512], P(None, 'dom'), may hold values from -144 to 144
- viscosity: float32 [2048], P('dom'), may hold values from 0.3 to 3
- mass_coef: float32 [2048], P('dom'), may hold values from 8 to 80
- element_order: int32 [8, 256], P('dom'), may hold values from 0 to 255, each once within a row
- owner: int32 [8, 256], P('dom'), may hold values from -1 to 7, as said below
Outputs:
- fields: float32 [4, 2048, 512], P('grp', 'dom')
Inputs may be any that keep to these rules, and one draw needn't show every extreme that they name: `element_order`: row d gives each element slot of partition d its cell in the partition's brick of 8 x 8 x 4 elements, every cell once. -1 marks an element that is not analysed; at most 32 elements of one partition have the same owner, and some owner gets exactly 32 from every partition.
All inputs are finite; a program needn't handle non-finite values.
Results may differ from a plain program's by a relative error of at most 0.00037.
Values may be sent and summed in bfloat16 or wider, within the bound.
No kernel may reach another device: no remote copies, remote signals or barrier semaphores. Data moves between devices by JAX's collectives and lax.ppermute only.
A program may use at most 64 MiB of HBM per device.

v0:
```python
import jax
import jax.numpy as jnp
import numpy as np
from jax import lax
from jax.experimental import pallas as pl
from jax.experimental.pallas import tpu as pltpu
from jax.sharding import PartitionSpec as P

NP = 8
BX = 8
BY = 8
ITERS = 4
SWEEPS = 4
FACE = NP * NP
LAYER = BX * BY
TILE = 2 * LAYER
F32 = jnp.float32
BF16 = jnp.bfloat16


def legendre_values(points, node_count):
    legendre = np.zeros((points.shape[0], node_count))
    legendre[:, 0] = 1.0
    legendre[:, 1] = points
    for poly_order in range(2, node_count):
        legendre[:, poly_order] = (
            (2 * poly_order - 1) * points * legendre[:, poly_order - 1]
            - (poly_order - 1) * legendre[:, poly_order - 2]
        ) / poly_order
    return legendre


def lobatto_table(node_count):
    degree = node_count - 1
    points = np.cos(np.pi * np.arange(node_count) / degree)
    for attempt in range(60):
        legendre = legendre_values(points, node_count)
        points = points - (points * legendre[:, degree] - legendre[:, degree - 1]) / (
            node_count * legendre[:, degree]
        )
    points = points[::-1].copy()
    end_values = legendre_values(points, node_count)[:, degree]
    weights = 2.0 / (degree * node_count * end_values * end_values)
    spacing = points[:, None] - points[None, :] + np.eye(node_count)
    diff_matrix = end_values[:, None] / end_values[None, :] / spacing
    diff_matrix = diff_matrix * (1.0 - np.eye(node_count))
    diff_matrix[0, 0] = -degree * node_count / 4.0
    diff_matrix[-1, -1] = degree * node_count / 4.0
    return (weights, diff_matrix)


def operator_tables(node_count):
    weights, diff_matrix = lobatto_table(node_count)
    identity = np.eye(node_count)
    weight_cube = (
        weights[:, None, None] * weights[None, :, None] * weights[None, None, :]
    ).reshape(-1)
    directional = [
        np.kron(identity, np.kron(identity, diff_matrix)),
        np.kron(identity, np.kron(diff_matrix, identity)),
        np.kron(diff_matrix, np.kron(identity, identity)),
    ]
    stiffness = np.zeros((node_count**3, node_count**3))
    for direction_matrix in directional:
        stiffness = stiffness + direction_matrix.T @ (weight_cube[:, None] * direction_matrix)
    return diff_matrix, weight_cube, stiffness


def split3_np(table):
    parts = []
    rest = np.asarray(table, np.float64)
    for _ in range(3):
        part = rest.astype(np.float32).astype(BF16)
        parts.append(part)
        rest = rest - part.astype(np.float64)
    return parts


def host_tables():
    diff_matrix, weight_cube, stiffness = operator_tables(NP)
    half = FACE * NP // 2
    flip = np.concatenate([np.arange(FACE) + FACE * k for k in range(NP - 1, NP // 2 - 1, -1)])
    top = stiffness[:half, :half]
    cross = stiffness[:half][:, flip]
    even = split3_np(0.5 * (top + cross))
    odd = split3_np(0.5 * (top - cross))
    kmat = np.stack(even + odd)
    diag = np.diag(stiffness)
    scaled = stiffness / np.sqrt(diag[:, None] * diag[None, :])
    bound = max(1.0, float(np.linalg.eigvalsh(scaled)[-1]))
    cols = np.stack([weight_cube, diag]).astype(np.float32)
    cols = np.ascontiguousarray(np.broadcast_to(cols[:, :, None], cols.shape + (TILE,)))
    dcol = np.zeros((NP, NP, TILE), np.float32)
    for shift in range(NP):
        for row in range(NP):
            dcol[shift, row] = diff_matrix[row, (row + shift) % NP]
    return diff_matrix, kmat, cols, dcol, bound


def split3(value):
    high = value.astype(BF16)
    rest = value - high.astype(F32)
    mid = rest.astype(BF16)
    low = (rest - mid.astype(F32)).astype(BF16)
    return high, mid, low


def dot_nn(a, b):
    return jnp.dot(a, b, preferred_element_type=F32)


def dot_nt(a, b):
    return lax.dot_general(a, b, (((1,), (1,)), ((), ())), preferred_element_type=F32)


def iota(shape, dim):
    return lax.broadcasted_iota(jnp.int32, shape, dim)


def wide(col, lanes):
    return jnp.concatenate([col] * (lanes // col.shape[1]), axis=1)


def prep_kernel(comp_ref, force_ref, order_ref, coef_ref, cols_ref, pack_ref):
    elems = order_ref.shape[1]
    nodes = force_ref.shape[2]
    cell_by_slot = (iota((elems, elems), 0) == order_ref[...]).astype(F32)
    perm = jnp.transpose(cell_by_slot).astype(BF16)
    chunk = 128
    for at in range(0, nodes, chunk):
        piece = jnp.transpose(force_ref[0, :, at : at + chunk])
        high, mid, low = split3(piece)
        moved = dot_nn(high, perm) + dot_nn(mid, perm) + dot_nn(low, perm)
        pack_ref[at : at + chunk, :] = wide(cols_ref[0, at : at + chunk, :], elems) * moved
    high, mid, low = split3(coef_ref[...])
    pack_ref[nodes:, :] = dot_nn(high, perm) + dot_nn(mid, perm) + dot_nn(low, perm)


def place_kernel(cap, order_ref, owner_ref, place_ref):
    elems = order_ref.shape[1]
    owners = elems // cap
    rows = max(8, owners)
    owner_row = owner_ref[...]
    match = (iota((rows, elems), 0) == owner_row).astype(F32)
    before = (iota((elems, elems), 0) < iota((elems, elems), 1)).astype(BF16)
    running = dot_nn(match.astype(BF16), before)
    rank = jnp.sum(match * running, axis=0, keepdims=True).astype(jnp.int32)
    dest = jnp.where(owner_row >= 0, owner_row * cap + rank, -1)
    to_dest = (iota((elems, elems), 0) == dest).astype(BF16)
    cell_by_slot = (iota((elems, elems), 0) == order_ref[...]).astype(BF16)
    place_ref[...] = dot_nt(to_dest, cell_by_slot).astype(BF16)


def lane_masks(rows):
    lane = iota((rows, TILE), 1)
    x_pos = lane % BX
    y_pos = lane // BX % BY
    return x_pos < BX - 1, x_pos > 0, y_pos < BY - 1, y_pos > 0, lane < LAYER


def pair(first, second, keep, back, stride, scale):
    up = pltpu.roll(first, TILE - stride, 1)
    down = pltpu.roll(second, stride, 1)
    if scale is None:
        return first + jnp.where(back, down, 0.0), second + jnp.where(keep, up, 0.0)
    return (
        jnp.where(back, scale * (first + down), first),
        jnp.where(keep, scale * (second + up), second),
    )


def share_xy(ref, tiles, scale=None):
    x_keep, x_back, y_keep, y_back, _ = lane_masks(FACE)
    y_keep, y_back = y_keep[:NP], y_back[:NP]
    for t in tiles:
        low = ref[t, pl.ds(0, FACE, stride=NP), :]
        high = ref[t, pl.ds(NP - 1, FACE, stride=NP), :]
        low, high = pair(low, high, x_keep, x_back, 1, scale)
        ref[t, pl.ds(0, FACE, stride=NP), :] = low
        ref[t, pl.ds(NP - 1, FACE, stride=NP), :] = high
        for k in range(NP):
            first = pl.ds(k * FACE, NP)
            last = pl.ds(k * FACE + FACE - NP, NP)
            low, high = pair(ref[t, first, :], ref[t, last, :], y_keep, y_back, BX, scale)
            ref[t, first, :] = low
            ref[t, last, :] = high


def load_block(ref, n, rows):
    return jnp.concatenate([ref[2 * n, rows, :], ref[2 * n + 1, rows, :]], axis=1)


def save_block(ref, n, rows, value):
    ref[2 * n, rows, :] = value[:, :TILE]
    ref[2 * n + 1, rows, :] = value[:, TILE:]


def share_z(ref, tiles):
    lower = lane_masks(FACE)[4]
    first = pl.ds(0, FACE)
    last = pl.ds((NP - 1) * FACE, FACE)
    lows = [ref[t, first, :] for t in tiles]
    highs = [ref[t, last, :] for t in tiles]
    low_roll = [pltpu.roll(v, LAYER, 1) for v in lows] + [jnp.zeros((FACE, TILE), F32)]
    high_roll = [jnp.zeros((FACE, TILE), F32)] + [pltpu.roll(v, LAYER, 1) for v in highs]
    for n, t in enumerate(tiles):
        up = jnp.where(lower, low_roll[n], low_roll[n + 1])
        down = jnp.where(lower, high_roll[n], high_roll[n + 1])
        ref[t, last, :] = highs[n] + up
        ref[t, first, :] = lows[n] + down


def krylov_kernel(
    diff, bound, meta_ref, own_ref, a_ref, b_ref, kmat_ref, cols_ref,
    basis_ref, near_ref, face_ref, dots_ref,
    work, coef, inv, vec, ghost, even, odd, prod,
):
    nodes = cols_ref.shape[1]
    elems = own_ref.shape[1]
    half = nodes // 2
    steps = ITERS
    odd_part = meta_ref[1] > 0
    wide_tile = pl.ds(0, TILE)
    high_tile = pl.ds(TILE, TILE)

    def gather(rows, out_own, out_near, out_far):
        out_own(own_ref[rows, :])
        a_low, a_high = a_ref[rows, wide_tile], a_ref[rows, high_tile]
        b_low, b_high = b_ref[rows, wide_tile], b_ref[rows, high_tile]
        out_near(
            jnp.where(odd_part, a_high, b_high), jnp.where(odd_part, b_low, a_low)
        )
        out_far(
            jnp.where(odd_part, a_low, b_low), jnp.where(odd_part, b_high, a_high)
        )

    def store(ref, n, rows):
        def put(*parts):
            save_block(ref, n, rows, parts[0] if len(parts) == 1 else jnp.concatenate(parts, axis=1))
        return put

    def store_coef(n):
        def put(*parts):
            coef[n] = parts[0] if len(parts) == 1 else jnp.concatenate(parts, axis=1)
        return put

    tail = pl.ds(nodes, own_ref.shape[0] - nodes)
    gather(tail, store_coef(0), store_coef(1), store_coef(2))

    @pl.loop(0, NP)
    def _(k):
        rows = pl.ds(pl.multiple_of(k * FACE, FACE), FACE)
        gather(rows, store(work, 0, rows), store(work, 1, rows), store(work, 2, rows))
        w_col = wide(cols_ref[0, rows, :], elems)
        d_col = wide(cols_ref[1, rows, :], elems)
        for n in range(3):
            save_block(inv, n, rows, coef[n, 0:1, :] * d_col + coef[n, 1:2, :] * w_col)

    far_tiles = [4, 2, 0, 1, 3, 5]
    near_tiles = far_tiles[1:5]
    share_xy(work, far_tiles)
    share_z(work, far_tiles)
    share_xy(inv, far_tiles)
    share_z(inv, far_tiles)

    @pl.loop(0, NP)
    def _(k):
        rows = pl.ds(pl.multiple_of(k * FACE, FACE), FACE)
        for n in range(3):
            total = load_block(inv, n, rows)
            recip = jnp.where(total > 0.0, 1.0 / total, 0.0)
            save_block(inv, n, rows, recip)
            value = recip * load_block(work, n, rows)
            if n == 0:
                basis_ref[0, rows, :] = value
            elif n == 1:
                ghost[0, rows, :] = value
            else:
                vec[rows, :] = value

    def vector(m, n, rows):
        if n == 0:
            return basis_ref[m, rows, :]
        return ghost[m, rows, :] if n == 1 else vec[rows, :]

    dots_ref[...] = jnp.zeros_like(dots_ref)

    def fold(value):
        rows, lanes = value.shape
        total = jnp.sum(value.reshape(rows // 8, 8, lanes), axis=0)
        return sum(total[:, at : at + TILE] for at in range(0, lanes, TILE))

    def apply(m, n):
        @pl.loop(0, NP // 2)
        def _(k):
            top = pl.ds(pl.multiple_of(k * FACE, FACE), FACE)
            bottom = pl.ds(pl.multiple_of((NP - 1 - k) * FACE, FACE), FACE)
            v_top = vector(m, n, top)
            v_bottom = vector(m, n, bottom)
            for part, ref in ((v_top + v_bottom, even), (v_top - v_bottom, odd)):
                high, mid, low = split3(part)
                ref[0, top, :] = high
                ref[1, top, :] = mid
                ref[2, top, :] = low

        for parity, ref in ((0, even), (1, odd)):
            base = 3 * parity
            prod[parity] = (
                dot_nn(kmat_ref[base], ref[2])
                + dot_nn(kmat_ref[base + 1], ref[1])
                + dot_nn(kmat_ref[base + 2], ref[0])
                + dot_nn(kmat_ref[base], ref[1])
                + dot_nn(kmat_ref[base + 1], ref[0])
                + dot_nn(kmat_ref[base], ref[0])
            )

        @pl.loop(0, NP // 2)
        def _(k):
            top = pl.ds(pl.multiple_of(k * FACE, FACE), FACE)
            bottom = pl.ds(pl.multiple_of((NP - 1 - k) * FACE, FACE), FACE)
            p_even = prod[0, top, :]
            p_odd = prod[1, top, :]
            w_top = wide(cols_ref[0, top, :], elems)
            w_bottom = wide(cols_ref[0, bottom, :], elems)
            visc = coef[n, 0:1, :]
            mass = coef[n, 1:2, :]
            q_top = visc * (p_even + p_odd) + mass * (w_top * vector(m, n, top))
            q_bottom = visc * (p_even - p_odd) + mass * (w_bottom * vector(m, n, bottom))
            if m + 1 < steps:
                save_block(work, n, top, q_top)
                save_block(work, n, bottom, q_bottom)
            if n == 0:
                for i in range(m + 1):
                    dots_ref[m * (m + 1) // 2 + i] += fold(
                        basis_ref[i, top, :] * q_top + basis_ref[i, bottom, :] * q_bottom
                    )
                at = steps * (steps + 1) // 2 + m
                dots_ref[at] += fold(
                    basis_ref[m, top, :] * own_ref[top, :]
                    + basis_ref[m, bottom, :] * own_ref[bottom, :]
                )

    for m in range(steps):
        if m + 1 == steps:
            apply(m, 0)
            continue
        blocks = (0, 1, 2) if m == 0 else (0, 1)
        for n in blocks:
            apply(m, n)
        tiles = far_tiles if m == 0 else near_tiles
        share_xy(work, tiles)
        share_z(work, tiles)
        outs = (0, 1) if m + 2 < steps else (0,)

        @pl.loop(0, NP)
        def _(k):
            rows = pl.ds(pl.multiple_of(k * FACE, FACE), FACE)
            for n in outs:
                value = (2.0 / bound) * (load_block(inv, n, rows) * load_block(work, n, rows)) - vector(m, n, rows)
                if m > 0:
                    value = value + value - vector(m - 1, n, rows)
                if n == 0:
                    basis_ref[m + 1, rows, :] = value
                else:
                    ghost[m + 1, rows, :] = value

    def plane(load, row):
        total = None
        for k in range(NP):
            term = float(diff[row, k]) * load(k)
            total = term if total is None else total + term
        return total

    lower = lane_masks(FACE)[4]

    def rows_of(k):
        return pl.ds(k * FACE, FACE)

    last = steps - 1
    bottom = plane(lambda k: basis_ref[last, rows_of(k), wide_tile], 0)
    top = plane(lambda k: basis_ref[last, rows_of(k), high_tile], NP - 1)
    face_ref[...] = jnp.where(lower, bottom, top)
    for m in range(steps - 1):
        below = plane(lambda k: ghost[m, rows_of(k), wide_tile], NP - 1)
        above = plane(lambda k: ghost[m, rows_of(k), high_tile], 0)
        near_ref[m] = jnp.where(lower, above, below)


def solve_coefficients(sums):
    size = ITERS
    gram = {}
    for j in range(size):
        for i in range(j + 1):
            at = j * (j + 1) // 2 + i
            gram[j, i] = sums[at : at + 1]
    at = size * (size + 1) // 2
    right = [sums[at + i : at + i + 1] for i in range(size)]
    lower, recip = {}, []
    reduced = {}
    for k in range(size):
        for i in range(k, size):
            value = gram[i, k]
            for m in range(k):
                value = value - lower[i, m] * reduced[k, m]
            reduced[i, k] = value
        pivot = reduced[k, k]
        usable = pivot > 1e-7 * gram[k, k]
        inverse = jnp.where(usable, 1.0 / jnp.where(usable, pivot, 1.0), 0.0)
        recip.append(inverse)
        for i in range(k + 1, size):
            lower[i, k] = reduced[i, k] * inverse
    for k in range(size):
        for m in range(k):
            right[k] = right[k] - lower[k, m] * right[m]
    out = [None] * size
    for k in reversed(range(size)):
        value = right[k] * recip[k]
        for m in range(k + 1, size):
            value = value - lower[m, k] * out[m]
        out[k] = value
    return out


def gradient_kernel(
    diff, meta_ref, dots_ref, basis_ref, near_ref, fa_ref, fb_ref, dcol_ref,
    grad_ref, vel_ref, work,
):
    elems = basis_ref.shape[2]
    quarters = grad_ref.shape[0]
    quarter = grad_ref.shape[2]
    scalars = jnp.sum(dots_ref[...], axis=1, keepdims=True)
    weights = solve_coefficients(scalars)
    tiles = range(elems // TILE)

    @pl.loop(0, NP)
    def _(k):
        rows = pl.ds(pl.multiple_of(k * FACE, FACE), FACE)
        total = weights[0] * basis_ref[0, rows, :]
        for m in range(1, ITERS):
            total = total + weights[m] * basis_ref[m, rows, :]
        vel_ref[rows, :] = total

    lower = lane_masks(FACE)[4]
    x_keep, x_back, y_keep, y_back, _ = lane_masks(FACE)
    odd_part = meta_ref[1] > 0
    from_above = jnp.where(odd_part, fb_ref[...], fa_ref[...])
    from_below = jnp.where(odd_part, fa_ref[...], fb_ref[...])
    near = weights[ITERS - 1] * jnp.where(lower, from_above, from_below)
    for m in range(ITERS - 1):
        near = near + weights[m] * near_ref[m]
    near = pltpu.roll(near, LAYER, 1)

    def finish(direction, scale):
        share_xy(work, tiles, 0.5)
        if direction == 2:
            first = pl.ds(0, FACE)
            last = pl.ds((NP - 1) * FACE, FACE)
            lows = [work[t, first, :] for t in tiles]
            highs = [work[t, last, :] for t in tiles]
            low_roll = [pltpu.roll(v, LAYER, 1) for v in lows] + [near]
            high_roll = [near] + [pltpu.roll(v, LAYER, 1) for v in highs]
            count = len(tiles)
            for n in tiles:
                up = jnp.where(lower, low_roll[n], low_roll[n + 1])
                down = jnp.where(lower, high_roll[n], high_roll[n + 1])
                high_mean = 0.5 * (highs[n] + up)
                low_mean = 0.5 * (lows[n] + down)
                if n == count - 1:
                    edge = jnp.logical_and(jnp.logical_not(lower), meta_ref[3] > 0)
                    high_mean = jnp.where(edge, highs[n], high_mean)
                if n == 0:
                    edge = jnp.logical_and(lower, meta_ref[2] > 0)
                    low_mean = jnp.where(edge, lows[n], low_mean)
                work[n, last, :] = high_mean
                work[n, first, :] = low_mean
        for q in range(quarters):
            grad_ref[q, direction] = (load_block(work, 0, pl.ds(q * quarter, quarter)) * scale).astype(BF16)

    @pl.loop(0, NP)
    def _(k):
        rows = pl.ds(pl.multiple_of(k * FACE, FACE), FACE)
        value = vel_ref[rows, :].reshape(NP, NP, elems)
        total = wide(dcol_ref[0], elems)[None] * value
        for shift in range(1, NP):
            total = total + wide(dcol_ref[shift], elems)[None] * pltpu.roll(value, NP - shift, 1)
        save_block(work, 0, rows, total.reshape(FACE, elems))

    finish(0, 1.0 / NP)

    @pl.loop(0, NP)
    def _(k):
        rows = pl.ds(pl.multiple_of(k * FACE, FACE), FACE)
        value = vel_ref[rows, :].reshape(NP, NP, elems)
        for j in range(NP):
            total = float(diff[j, 0]) * value[0]
            for m in range(1, NP):
                total = total + float(diff[j, m]) * value[m]
            save_block(work, 0, pl.ds(pl.multiple_of(k * FACE + j * NP, NP), NP), total)

    finish(1, 1.0 / NP)

    @pl.loop(0, NP)
    def _(j):
        planes = [vel_ref[pl.ds(pl.multiple_of(m * FACE + j * NP, NP), NP), :] for m in range(NP)]
        for k in range(NP):
            total = float(diff[k, 0]) * planes[0]
            for m in range(1, NP):
                total = total + float(diff[k, m]) * planes[m]
            save_block(work, 0, pl.ds(pl.multiple_of(k * FACE + j * NP, NP), NP), total)

    finish(2, 1.0 / NP)


def slots_kernel(order_ref, vel_ref, out_ref):
    elems = order_ref.shape[1]
    cell_by_slot = (iota((elems, elems), 0) == order_ref[...]).astype(F32)
    pick = jnp.transpose(cell_by_slot).astype(BF16)
    high, mid, low = split3(vel_ref[...])
    out_ref[...] = dot_nt(pick, high) + dot_nt(pick, mid) + dot_nt(pick, low)


def middle_eigenvalue(jac):
    strain = [[0.5 * (jac[a][b] + jac[b][a]) for b in range(3)] for a in range(3)]
    spin = [[0.5 * (jac[a][b] - jac[b][a]) for b in range(3)] for a in range(3)]
    mat = [[None] * 3 for _ in range(3)]
    for a in range(3):
        for b in range(a, 3):
            total = strain[a][0] * strain[0][b] + spin[a][0] * spin[0][b]
            for c in (1, 2):
                total = total + strain[a][c] * strain[c][b] + spin[a][c] * spin[c][b]
            mat[a][b] = total
            mat[b][a] = total
    for _ in range(SWEEPS):
        for p, q, r in ((0, 1, 2), (0, 2, 1), (1, 2, 0)):
            pivot = mat[p][q]
            first, second = mat[p][p], mat[q][q]
            num = 2.0 * pivot
            den = first - second
            size = jnp.maximum(jnp.abs(num), jnp.abs(den))
            safe = jnp.where(size > 0.0, size, 1.0)
            num_s = num / safe
            den_s = den / safe
            inv_norm = lax.rsqrt(jnp.where(size > 0.0, num_s * num_s + den_s * den_s, 1.0))
            cos_two = jnp.where(size > 0.0, den_s * inv_norm, 1.0)
            sin_two = num_s * inv_norm
            big = jnp.sqrt(0.5 + 0.5 * jnp.abs(cos_two))
            small = 0.5 * sin_two / big
            forward = cos_two >= 0.0
            sign = jnp.where(num < 0.0, -1.0, 1.0)
            cosine = jnp.where(forward, big, jnp.abs(small))
            sine = jnp.where(forward, small, sign * big)
            cross = 2.0 * cosine * sine * pivot
            cc, ss = cosine * cosine, sine * sine
            side_p, side_q = mat[r][p], mat[r][q]
            mat[p][p] = cc * first + cross + ss * second
            mat[q][q] = ss * first - cross + cc * second
            zero = jnp.zeros_like(pivot)
            mat[p][q] = mat[q][p] = zero
            mat[r][p] = mat[p][r] = cosine * side_p + sine * side_q
            mat[r][q] = mat[q][r] = cosine * side_q - sine * side_p
    d0, d1, d2 = mat[0][0], mat[1][1], mat[2][2]
    largest = jnp.maximum(jnp.maximum(d0, d1), d2)
    smallest = jnp.minimum(jnp.minimum(d0, d1), d2)
    return d0 + d1 + d2 - largest - smallest


def vortex_kernel(grad_ref, place_ref, out_ref, value):
    rows_all = grad_ref.shape[2]
    step = 16

    @pl.loop(0, rows_all // step)
    def _(n):
        rows = pl.ds(pl.multiple_of(n * step, step), step)
        jac = [[grad_ref[c, d, rows, :].astype(F32) for d in range(3)] for c in range(3)]
        value[rows, :] = middle_eigenvalue(jac)

    high, mid, low = split3(value[...])
    place = place_ref[...]
    moved = dot_nt(place, high) + dot_nt(place, mid) + dot_nt(place, low)
    out_ref[...] = moved.reshape(out_ref.shape)


def final_kernel(meta_ref, vortex_ref, vel_ref, out_ref):
    quarters = vortex_ref.shape[0]
    quarter = vortex_ref.shape[2]

    @pl.when(meta_ref[4] > 0)
    def _():
        for q in range(quarters):
            out_ref[0, :, q * quarter : (q + 1) * quarter] = vortex_ref[q]

    @pl.when(meta_ref[4] == 0)
    def _():
        out_ref[0] = vel_ref[...]


def vmem():
    return pl.BlockSpec(memory_space=pltpu.VMEM)


def smem():
    return pl.BlockSpec(memory_space=pltpu.SMEM)


def cost(flops, size):
    return pl.CostEstimate(flops=flops, bytes_accessed=size, transcendentals=0)


def per_device(forcing, viscosity, mass_coef, element_order, owner):
    elems = viscosity.shape[0]
    nodes = forcing.shape[2]
    parts = lax.axis_size("dom")
    groups = lax.axis_size("grp")
    part = lax.axis_index("dom")
    group = lax.axis_index("grp")
    cap = elems // parts
    quarter = nodes // groups
    diff, kmat_np, cols_np, dcol_np, bound = host_tables()
    kmat = jnp.asarray(kmat_np, BF16)
    cols = jnp.asarray(cols_np)
    dcol = jnp.asarray(dcol_np)
    meta = jnp.stack(
        [
            jnp.minimum(group, 2),
            part % 2,
            (part == 0).astype(jnp.int32),
            (part == parts - 1).astype(jnp.int32),
            (group == groups - 1).astype(jnp.int32),
        ]
    ).astype(jnp.int32)
    coef = jnp.concatenate(
        [viscosity[None], mass_coef[None], jnp.zeros((6, elems), F32)], axis=0
    )
    sds = jax.ShapeDtypeStruct

    pack = pl.pallas_call(
        prep_kernel,
        grid_spec=pltpu.PrefetchScalarGridSpec(
            num_scalar_prefetch=1,
            grid=(1,),
            in_specs=[
                pl.BlockSpec((1, elems, nodes), lambda n, m: (m[0], 0, 0)),
                pl.BlockSpec((1, elems), lambda n, m: (0, 0)),
                pl.BlockSpec((8, elems), lambda n, m: (0, 0)),
                pl.BlockSpec((2, nodes, TILE), lambda n, m: (0, 0, 0)),
            ],
            out_specs=pl.BlockSpec((nodes + 8, elems), lambda n, m: (0, 0)),
        ),
        out_shape=sds((nodes + 8, elems), F32),
        cost_estimate=cost(10**9, 2 * 10**6),
        name="prep",
    )(meta, forcing, element_order, coef, cols)

    swap_a = [(i, i ^ 1) for i in range(parts) if i ^ 1 < parts]
    swap_b = [(i, ((i - 1) ^ 1) + 1) for i in range(1, parts - 1)]
    ghost_a = lax.ppermute(pack, "dom", swap_a)
    ghost_b = lax.ppermute(pack, "dom", swap_b)

    place = pl.pallas_call(
        lambda *refs: place_kernel(cap, *refs),
        in_specs=[vmem(), vmem()],
        out_specs=vmem(),
        out_shape=sds((elems, elems), BF16),
        cost_estimate=cost(10**9, 2 * 10**6),
        name="place",
    )(element_order, owner)

    basis, near, face, dots = pl.pallas_call(
        lambda *refs: krylov_kernel(diff, bound, *refs),
        in_specs=[smem()] + [vmem()] * 5,
        out_specs=[vmem()] * 4,
        out_shape=[
            sds((ITERS, nodes, elems), F32),
            sds((ITERS - 1, FACE, TILE), F32),
            sds((FACE, TILE), F32),
            sds((16, 8, TILE), F32),
        ],
        scratch_shapes=[
            pltpu.VMEM((6, nodes, TILE), F32),
            pltpu.VMEM((3, 8, elems), F32),
            pltpu.VMEM((6, nodes, TILE), F32),
            pltpu.VMEM((nodes, elems), F32),
            pltpu.VMEM((ITERS - 1, nodes, elems), F32),
            pltpu.VMEM((3, nodes // 2, elems), BF16),
            pltpu.VMEM((3, nodes // 2, elems), BF16),
            pltpu.VMEM((2, nodes // 2, elems), F32),
        ],
        cost_estimate=cost(10**10, 10**7),
        name="krylov",
    )(meta, pack, ghost_a, ghost_b, kmat, cols)

    message = jnp.concatenate([face, jnp.sum(dots, axis=1)], axis=0)
    face_a = lax.ppermute(message, "dom", swap_a)
    face_b = lax.ppermute(face, "dom", swap_b)
    sums = message[FACE:] + face_a[FACE:]
    reach = 2
    while reach < parts:
        sums = sums + lax.ppermute(sums, "dom", [(i, i ^ reach) for i in range(parts)])
        reach *= 2

    grads, vel = pl.pallas_call(
        lambda *refs: gradient_kernel(diff, *refs),
        in_specs=[smem()] + [vmem()] * 6,
        out_specs=[vmem()] * 2,
        out_shape=[sds((groups, 3, quarter, elems), BF16), sds((nodes, elems), F32)],
        scratch_shapes=[pltpu.VMEM((2, nodes, TILE), F32)],
        cost_estimate=cost(10**9, 4 * 10**6),
        name="gradient",
    )(meta, sums, basis, near, face_a[:FACE], face_b, dcol)

    exchanged = lax.all_to_all(grads, "grp", split_axis=0, concat_axis=0, tiled=True)

    vel_slot = pl.pallas_call(
        slots_kernel,
        in_specs=[vmem(), vmem()],
        out_specs=vmem(),
        out_shape=sds((elems, nodes), F32),
        cost_estimate=cost(10**9, 2 * 10**6),
        name="slots",
    )(element_order, vel)

    packed = pl.pallas_call(
        vortex_kernel,
        in_specs=[vmem(), vmem()],
        out_specs=vmem(),
        out_shape=sds((parts, cap, quarter), F32),
        scratch_shapes=[pltpu.VMEM((quarter, elems), F32)],
        cost_estimate=cost(10**9, 2 * 10**6),
        name="vortex",
    )(exchanged, place)

    padding = jnp.zeros(((groups - 1) * parts, cap, quarter), F32)
    received = lax.all_to_all(
        jnp.concatenate([padding, packed], 0),
        ("grp", "dom"),
        split_axis=0,
        concat_axis=0,
        tiled=True,
    )
    return pl.pallas_call(
        final_kernel,
        in_specs=[smem(), vmem(), vmem()],
        out_specs=vmem(),
        out_shape=sds((1, elems, nodes), F32),
        cost_estimate=cost(10**6, 2 * 10**6),
        name="final",
    )(meta, received.reshape(groups, elems, quarter), vel_slot)


def solution(mesh):
    in_specs = (P(None, "dom", None), P("dom"), P("dom"), P("dom", None), P("dom", None))
    out_specs = P("grp", "dom", None)
    return jax.shard_map(
        per_device, mesh=mesh, in_specs=in_specs, out_specs=out_specs, check_vma=False
    )
```

profile of v0, /device:TPU:0, one launch (start us, length us, event | category | flops | bytes accessed | tf_op | source)
XLA Modules:
  0.0 98.8 jit_solution(3215210168018595324)
XLA Ops:
  0.0 0.1 pad.5.clone
  0.1 1.4 %maximum_maximum_fusion.coef_ref = f32[8,256]{1,0:T(8,128)} fusion(f32[1,256]{1,0:T(1,128)} %bitcast.9, f32[1,256]{1,0:T(1,128)} %bitcast.10, f32[8]{0:T(128)S(1)} %pad.5.clone), kind=kLoop, calls=%fused_computation.2 | loop fusion | flops 4096 | bytes 10272 | tf_op jit(solution)/shard_map/concatenate | solution.py:631
  1.4 0.6 stack.35.comp_ref.refs_0_.meta_ref
  2.0 3.2 %prep.1.refs_1_ = f32[520,256]{1,0:T(8,128)} custom-call(s32[5]{0:T(128)} %stack.35.comp_ref.refs_0_.meta_ref, f32[3,256,512]{2,1,0:T(8,128)} %force_ref.1, s32[1,256]{1,0:T(1,128)} %order_ref.3, f32[8,256]{1,0:T(8,128)} %maximum_maximum_fusion.coef_ref, f32[2,512,128]{2,1,0:T(8,128)} %constant.37.clone.cols_ref.refs_5_), custom_call_target="tpu_custom_call" | custom-call | flops 1000000000 | bytes 2000000 | tf_op jit(solution)/shard_map/prep/pallas_call | solution.py:636
  5.2 0.5 collective-permute-start
  5.7 0.7 collective-permute-start.1
  6.4 1.1 %collective-permute-done.refs_2_ = f32[520,256]{1,0:T(8,128)S(1)} collective-permute-done((f32[520,256]{1,0:T(8,128)}, f32[520,256]{1,0:T(8,128)S(1)}, u32[]{:S(2)}, u32[]{:S(2)}) %collective-permute-start) | collective-permute-done | bytes 532512 | tf_op jit(solution)/shard_map/ppermute | solution.py:656
  7.5 0.0 copy-start.2
  7.5 0.0 collective-permute-done.1.refs_3_
  7.5 0.8 copy-done.2
  8.3 0.0 copy-start.3
  8.3 0.8 copy-done.3
  9.1 14.9 %krylov.1 = (f32[4,512,256]{2,1,0:T(8,128)}, f32[3,64,128]{2,1,0:T(8,128)}, f32[64,128]{1,0:T(8,128)}, f32[16,8,128]{2,1,0:T(8,128)}) custom-call(s32[5]{0:T(128)} %stack.35.comp_ref.refs_0_.meta_ref, f32[520,256]{1,0:T(8,128)} %prep.1.refs_1_, f32[520,256]{1,0:T(8,128)} %copy-done.2, f32[520,256]{1,0:T(8,128)} %copy-done.3, ...), custom_call_target="tpu_custom_call" | custom-call | flops 10000000000 | bytes 10000000 | tf_op jit(solution)/shard_map/krylov/pallas_call | solution.py:668
  24.0 0.9 reduce_sum.9
  24.9 0.8 pad_maximum_fusion
  25.7 9.2 %collective-permute-start.2 = (f32[80,128]{1,0:T(8,128)S(1)}, f32[80,128]{1,0:T(8,128)S(1)}, u32[]{:S(2)}, u32[]{:S(2)}) collective-permute-start(f32[80,128]{1,0:T(8,128)S(1)} %pad_maximum_fusion), channel_id=1, source_target_pairs={{0,1},{1,0},{2,3},{3,2},{4,5},{5,4},{6,7},{7,6},{8,9},{9,8},{10,11... | collective-permute-start | bytes 122888 | tf_op jit(solution)/shard_map/ppermute | solution.py:693
  34.8 0.7 collective-permute-start.5
  35.5 0.2 collective-permute-done.2
  35.7 3.3 %collective-permute-start.3 = (f32[16,128]{1,0:T(8,128)S(1)}, f32[16,128]{1,0:T(8,128)S(1)}, u32[]{:S(2)}, u32[]{:S(2)}) collective-permute-start(f32[16,128]{1,0:T(8,128)S(1)} %slice_add_fusion), channel_id=1, source_target_pairs={{0,2},{1,3},{2,0},{3,1},{4,6},{5,7},{6,4},{7,5},{8,10},{9,11},{10,... | collective-permute-start | bytes 24584 | tf_op jit(solution)/shard_map/ppermute | solution.py:698
  39.0 2.1 %collective-permute-done.3 = f32[16,128]{1,0:T(8,128)S(1)} collective-permute-done((f32[16,128]{1,0:T(8,128)S(1)}, f32[16,128]{1,0:T(8,128)S(1)}, u32[]{:S(2)}, u32[]{:S(2)}) %collective-permute-start.3) | collective-permute-done | bytes 8224 | tf_op jit(solution)/shard_map/ppermute | solution.py:698
  41.0 2.6 %collective-permute-start.4 = (f32[16,128]{1,0:T(8,128)S(1)}, f32[16,128]{1,0:T(8,128)S(1)}, u32[]{:S(2)}, u32[]{:S(2)}) collective-permute-start(f32[16,128]{1,0:T(8,128)S(1)} %add.17), channel_id=1, source_target_pairs={{0,4},{1,5},{2,6},{3,7},{4,0},{5,1},{6,2},{7,3},{8,12},{9,13},{10,... | collective-permute-start | bytes 24584 | tf_op jit(solution)/shard_map/ppermute | solution.py:698
  43.7 0.6 slice.9.refs_4_
  44.3 1.3 %collective-permute-done.4 = f32[16,128]{1,0:T(8,128)S(1)} collective-permute-done((f32[16,128]{1,0:T(8,128)S(1)}, f32[16,128]{1,0:T(8,128)S(1)}, u32[]{:S(2)}, u32[]{:S(2)}) %collective-permute-start.4) | collective-permute-done | bytes 8224 | tf_op jit(solution)/shard_map/ppermute | solution.py:698
  45.6 0.6 add.18.refs_1_
  46.2 0.0 collective-permute-done.5.refs_5_
  46.2 0.0 copy-start.4
  46.2 0.6 copy-done.4
  46.8 4.9 %gradient.1 = (bf16[4,3,128,256]{3,2,1,0:T(8,128)(2,1)}, f32[512,256]{1,0:T(8,128)}) custom-call(s32[5]{0:T(128)} %stack.35.comp_ref.refs_0_.meta_ref, f32[16,128]{1,0:T(8,128)} %add.18.refs_1_, f32[4,512,256]{2,1,0:T(8,128)} %get-tuple-element.13.refs_2_, f32[3,64,128]{2,1,0:T(8,128)} %get-tuple-element.14.refs_3_, f32[64,128]{1,0:T(8,128)} %slice.9.refs_4_, ...), custom_call_target="tpu_custom_call" | custom-call | flops 1000000000 | bytes 4000000 | tf_op jit(solution)/shard_map/gradient/pallas_call | solution.py:701
  51.7 3.8 %all-to-all-start = ((bf16[4,3,128,256]{3,2,1,0:T(8,128)(2,1)}), bf16[4,3,128,256]{3,2,1,0:T(8,128)(2,1)S(1)}, u32[]{:S(2)}, u32[]{:S(2)}) async-start(bf16[4,3,128,256]{3,2,1,0:T(8,128)(2,1)} %get-tuple-element.15), calls=%async_computation | async-start | bytes 1572864 | tf_op jit(solution)/shard_map/all_to_all | solution.py:711
  55.5 1.7 %place.1.place_ref = bf16[256,256]{1,0:T(8,128)(2,1)} custom-call(s32[1,256]{1,0:T(1,128)} %order_ref.3, s32[1,256]{1,0:T(1,128)} %refs_1_.1), custom_call_target="tpu_custom_call" | custom-call | flops 1000000000 | bytes 2000000 | tf_op jit(solution)/shard_map/place/pallas_call | solution.py:659
  57.2 8.7 %all-to-all-done.grad_ref = bf16[4,3,128,256]{3,2,1,0:T(8,128)(2,1)S(1)} async-done(((bf16[4,3,128,256]{3,2,1,0:T(8,128)(2,1)}), bf16[4,3,128,256]{3,2,1,0:T(8,128)(2,1)S(1)}, u32[]{:S(2)}, u32[]{:S(2)}) %all-to-all-start) | async-done | bytes 786464 | tf_op jit(solution)/shard_map/all_to_all | solution.py:711
  65.8 0.0 copy-start.1
  65.8 0.9 copy-done.1
  66.8 7.4 %vortex.1 = f32[8,32,128]{2,1,0:T(8,128)} custom-call(bf16[4,3,128,256]{3,2,1,0:T(8,128)(2,1)} %copy-done.1, bf16[256,256]{1,0:T(8,128)(2,1)} %place.1.place_ref), custom_call_target="tpu_custom_call" | custom-call | flops 1000000000 | bytes 2000000 | tf_op jit(solution)/shard_map/vortex/pallas_call | solution.py:722
  74.2 1.8 %concatenate.11 = f32[32,32,128]{2,1,0:T(8,128)} pad(f32[8,32,128]{2,1,0:T(8,128)} %vortex.1, f32[]{:T(128)} %constant.35.clone.1), padding=24_0x0_0x0_0 | pad | bytes 655364 | tf_op jit(solution)/shard_map/concatenate | solution.py:734
  76.0 3.7 %all-to-all-start.1 = ((f32[32,32,128]{2,1,0:T(8,128)}), f32[32,32,128]{2,1,0:T(8,128)S(1)}, u32[]{:S(2)}, u32[]{:S(2)}) async-start(f32[32,32,128]{2,1,0:T(8,128)} %concatenate.11), calls=%async_computation.1 | async-start | bytes 1048576 | tf_op jit(solution)/shard_map/all_to_all | solution.py:733
  79.7 2.3 %slots.1.vel_ref = f32[256,512]{1,0:T(8,128)} custom-call(s32[1,256]{1,0:T(1,128)} %order_ref.3, f32[512,256]{1,0:T(8,128)} %get-tuple-element.16.vel_ref), custom_call_target="tpu_custom_call" | custom-call | flops 1000000000 | bytes 2000000 | tf_op jit(solution)/shard_map/slots/pallas_call | solution.py:713
  82.0 13.9 %all-to-all-done.1 = f32[32,32,128]{2,1,0:T(8,128)S(1)} async-done(((f32[32,32,128]{2,1,0:T(8,128)}), f32[32,32,128]{2,1,0:T(8,128)S(1)}, u32[]{:S(2)}, u32[]{:S(2)}) %all-to-all-start.1) | async-done | bytes 524320 | tf_op jit(solution)/shard_map/all_to_all | solution.py:733
  95.9 0.0 copy-start
  95.9 0.8 copy-done
  96.7 2.0 %final.1 = f32[1,256,512]{2,1,0:T(8,128)} custom-call(s32[5]{0:T(128)} %stack.35.comp_ref.refs_0_.meta_ref, f32[4,256,128]{2,1,0:T(8,128)} %bitcast.8, f32[256,512]{1,0:T(8,128)} %slots.1.vel_ref), custom_call_target="tpu_custom_call" | custom-call | flops 1000000 | bytes 2000000 | tf_op jit(solution)/shard_map/final/pallas_call | solution.py:740
  (3 shorter events, 0.0 us)
Async XLA Ops:
  5.2 2.3 %collective-permute-start = (f32[520,256]{1,0:T(8,128)}, f32[520,256]{1,0:T(8,128)S(1)}, u32[]{:S(2)}, u32[]{:S(2)}) collective-permute-start(f32[520,256]{1,0:T(8,128)} %prep.1.refs_1_), channel_id=1, source_target_pairs={{0,1},{1,0},{2,3},{3,2},{4,5},{5,4},{6,7},{7,6},{8,9},{9,8},{10,11... | collective-permute-start | bytes 1597448 | tf_op jit(solution)/shard_map/ppermute | solution.py:656
  5.7 1.8 %collective-permute-start.1 = (f32[520,256]{1,0:T(8,128)}, f32[520,256]{1,0:T(8,128)S(1)}, u32[]{:S(2)}, u32[]{:S(2)}) collective-permute-start(f32[520,256]{1,0:T(8,128)} %prep.1.refs_1_), channel_id=1, source_target_pairs={{1,2},{2,1},{3,4},{4,3},{5,6},{6,5},{9,10},{10,9},{11,12},{12,11},... | collective-permute-start | bytes 1597448 | tf_op jit(solution)/shard_map/ppermute | solution.py:657
  7.5 0.8 copy-start.2
  8.3 0.8 copy-start.3
  25.7 10.0 %collective-permute-start.2 = (f32[80,128]{1,0:T(8,128)S(1)}, f32[80,128]{1,0:T(8,128)S(1)}, u32[]{:S(2)}, u32[]{:S(2)}) collective-permute-start(f32[80,128]{1,0:T(8,128)S(1)} %pad_maximum_fusion), channel_id=1, source_target_pairs={{0,1},{1,0},{2,3},{3,2},{4,5},{5,4},{6,7},{7,6},{8,9},{9,8},{10,11... | collective-permute-start | bytes 122888 | tf_op jit(solution)/shard_map/ppermute | solution.py:693
  34.8 11.4 %collective-permute-start.5 = (f32[64,128]{1,0:T(8,128)}, f32[64,128]{1,0:T(8,128)S(1)}, u32[]{:S(2)}, u32[]{:S(2)}) collective-permute-start(f32[64,128]{1,0:T(8,128)} %get-tuple-element.12), channel_id=1, source_target_pairs={{1,2},{2,1},{3,4},{4,3},{5,6},{6,5},{9,10},{10,9},{11,12},{12,11},... | collective-permute-start | bytes 98312 | tf_op jit(solution)/shard_map/ppermute | solution.py:694
  35.7 5.3 %collective-permute-start.3 = (f32[16,128]{1,0:T(8,128)S(1)}, f32[16,128]{1,0:T(8,128)S(1)}, u32[]{:S(2)}, u32[]{:S(2)}) collective-permute-start(f32[16,128]{1,0:T(8,128)S(1)} %slice_add_fusion), channel_id=1, source_target_pairs={{0,2},{1,3},{2,0},{3,1},{4,6},{5,7},{6,4},{7,5},{8,10},{9,11},{10,... | collective-permute-start | bytes 24584 | tf_op jit(solution)/shard_map/ppermute | solution.py:698
  41.0 4.5 %collective-permute-start.4 = (f32[16,128]{1,0:T(8,128)S(1)}, f32[16,128]{1,0:T(8,128)S(1)}, u32[]{:S(2)}, u32[]{:S(2)}) collective-permute-start(f32[16,128]{1,0:T(8,128)S(1)} %add.17), channel_id=1, source_target_pairs={{0,4},{1,5},{2,6},{3,7},{4,0},{5,1},{6,2},{7,3},{8,12},{9,13},{10,... | collective-permute-start | bytes 24584 | tf_op jit(solution)/shard_map/ppermute | solution.py:698
  46.2 0.6 copy-start.4
  51.7 14.1 %all-to-all-start = ((bf16[4,3,128,256]{3,2,1,0:T(8,128)(2,1)}), bf16[4,3,128,256]{3,2,1,0:T(8,128)(2,1)S(1)}, u32[]{:S(2)}, u32[]{:S(2)}) async-start(bf16[4,3,128,256]{3,2,1,0:T(8,128)(2,1)} %get-tuple-element.15), calls=%async_computation | async-start | bytes 1572864 | tf_op jit(solution)/shard_map/all_to_all | solution.py:711
  65.8 0.9 copy-start.1
  76.0 20.0 %all-to-all-start.1 = ((f32[32,32,128]{2,1,0:T(8,128)}), f32[32,32,128]{2,1,0:T(8,128)S(1)}, u32[]{:S(2)}, u32[]{:S(2)}) async-start(f32[32,32,128]{2,1,0:T(8,128)} %concatenate.11), calls=%async_computation.1 | async-start | bytes 1048576 | tf_op jit(solution)/shard_map/all_to_all | solution.py:733
  95.9 0.8 copy-start
where the time goes:
time: 99.4 us; the launch traced here: 98.8 us
  Pallas kernels  36.6 us (37%)
  waiting for transfers between devices  27.3 us (27%)
  starting transfers between devices  24.4 us (25%)
  local copies, waits for them, and re-layouts  6.95 us (7%)
  other arithmetic  3.59 us (4%)
    pallas_call x1, Pallas kernels, per_device(): pl.pallas_call(lambda *refs: krylov_kernel(diff, bound, *refs), in_specs=...  14.9 us
    all_to_all x1, waiting for transfers between devices, per_device(): lax.all_to_all(jnp.concatenate([padding, packed], 0), ('grp', 'dom'), spl...  13.9 us
    ppermute x1, starting transfers between devices, per_device(): face_a = lax.ppermute(message, 'dom', swap_a)  9.17 us
    all_to_all x1, waiting for transfers between devices, per_device(): lax.all_to_all(grads, 'grp', split_axis=0, concat_axis=0, tiled=True)  8.68 us
    pallas_call x1, Pallas kernels, per_device(): pl.pallas_call(vortex_kernel, in_specs=[vmem(), vmem()], out_specs=vmem()...  7.45 us
    ppermute x2, starting transfers between devices, per_device(): lax.ppermute(sums, 'dom', [(i, i ^ reach) for i in range(parts)])  5.89 us
    pallas_call x1, Pallas kernels, per_device(): pl.pallas_call(lambda *refs: gradient_kernel(diff, *refs), in_specs=[smem...  4.92 us
    unnamed x10, local copies, waits for them, and re-layouts  3.92 us
  transfers between devices with their start and end apart: 8, of which 6 were waited for; matrix products, arithmetic and copies ran while one was open for 1% of the time, Pallas kernels for 4%

commit v1 on v0

--- a/solution.py
+++ b/solution.py
@@ -121,19 +121,24 @@
     return jnp.concatenate([col] * (lanes // col.shape[1]), axis=1)
 
 
-def prep_kernel(comp_ref, force_ref, order_ref, coef_ref, cols_ref, pack_ref):
+def prep_kernel(force_any, order_ref, visc_ref, mass_ref, cols_ref, pack_ref, force_ref, sem):
     elems = order_ref.shape[1]
-    nodes = force_ref.shape[2]
+    nodes = force_any.shape[2]
+    component = jnp.minimum(lax.axis_index("grp"), 2)
+    fetch = pltpu.make_async_copy(force_any.at[component], force_ref, sem)
+    fetch.start()
     cell_by_slot = (iota((elems, elems), 0) == order_ref[...]).astype(F32)
     perm = jnp.transpose(cell_by_slot).astype(BF16)
+    coef = jnp.concatenate([visc_ref[...], mass_ref[...], jnp.zeros((6, elems), F32)], axis=0)
+    high, mid, low = split3(coef)
+    pack_ref[nodes:, :] = dot_nn(high, perm) + dot_nn(mid, perm) + dot_nn(low, perm)
+    fetch.wait()
     chunk = 128
     for at in range(0, nodes, chunk):
-        piece = jnp.transpose(force_ref[0, :, at : at + chunk])
+        piece = jnp.transpose(force_ref[:, at : at + chunk])
         high, mid, low = split3(piece)
         moved = dot_nn(high, perm) + dot_nn(mid, perm) + dot_nn(low, perm)
         pack_ref[at : at + chunk, :] = wide(cols_ref[0, at : at + chunk, :], elems) * moved
-    high, mid, low = split3(coef_ref[...])
-    pack_ref[nodes:, :] = dot_nn(high, perm) + dot_nn(mid, perm) + dot_nn(low, perm)
 
 
 def place_kernel(cap, order_ref, owner_ref, place_ref):
@@ -211,15 +216,15 @@
 
 
 def krylov_kernel(
-    diff, bound, meta_ref, own_ref, a_ref, b_ref, kmat_ref, cols_ref,
-    basis_ref, near_ref, face_ref, dots_ref,
-    work, coef, inv, vec, ghost, even, odd, prod,
+    diff, bound, own_ref, a_ref, b_ref, kmat_ref, cols_ref,
+    basis_ref, near_ref, message_ref,
+    work, coef, inv, vec, ghost, even, odd, prod, dots_ref,
 ):
     nodes = cols_ref.shape[1]
     elems = own_ref.shape[1]
     half = nodes // 2
     steps = ITERS
-    odd_part = meta_ref[1] > 0
+    odd_part = lax.axis_index("dom") % 2 > 0
     wide_tile = pl.ds(0, TILE)
     high_tile = pl.ds(TILE, TILE)
 
@@ -298,16 +303,14 @@
             v_top = vector(m, n, top)
             v_bottom = vector(m, n, bottom)
             for part, ref in ((v_top + v_bottom, even), (v_top - v_bottom, odd)):
-                high, mid, low = split3(part)
+                high = part.astype(BF16)
                 ref[0, top, :] = high
-                ref[1, top, :] = mid
-                ref[2, top, :] = low
+                ref[1, top, :] = (part - high.astype(F32)).astype(BF16)
 
         for parity, ref in ((0, even), (1, odd)):
             base = 3 * parity
             prod[parity] = (
-                dot_nn(kmat_ref[base], ref[2])
-                + dot_nn(kmat_ref[base + 1], ref[1])
+                dot_nn(kmat_ref[base + 1], ref[1])
                 + dot_nn(kmat_ref[base + 2], ref[0])
                 + dot_nn(kmat_ref[base], ref[1])
                 + dot_nn(kmat_ref[base + 1], ref[0])
@@ -379,7 +382,8 @@
     last = steps - 1
     bottom = plane(lambda k: basis_ref[last, rows_of(k), wide_tile], 0)
     top = plane(lambda k: basis_ref[last, rows_of(k), high_tile], NP - 1)
-    face_ref[...] = jnp.where(lower, bottom, top)
+    message_ref[:FACE] = jnp.where(lower, bottom, top)
+    message_ref[FACE:] = jnp.sum(dots_ref[...], axis=1)
     for m in range(steps - 1):
         below = plane(lambda k: ghost[m, rows_of(k), wide_tile], NP - 1)
         above = plane(lambda k: ghost[m, rows_of(k), high_tile], 0)
@@ -422,13 +426,15 @@
 
 
 def gradient_kernel(
-    diff, meta_ref, dots_ref, basis_ref, near_ref, fa_ref, fb_ref, dcol_ref,
+    diff, sum_a_ref, sum_b_ref, basis_ref, near_ref, fa_ref, fb_ref, dcol_ref,
     grad_ref, vel_ref, work,
 ):
     elems = basis_ref.shape[2]
     quarters = grad_ref.shape[0]
     quarter = grad_ref.shape[2]
-    scalars = jnp.sum(dots_ref[...], axis=1, keepdims=True)
+    scalars = jnp.sum(sum_a_ref[...] + sum_b_ref[...], axis=1, keepdims=True)
+    part = lax.axis_index("dom")
+    parts = lax.axis_size("dom")
     weights = solve_coefficients(scalars)
     tiles = range(elems // TILE)
 
@@ -442,9 +448,9 @@
 
     lower = lane_masks(FACE)[4]
     x_keep, x_back, y_keep, y_back, _ = lane_masks(FACE)
-    odd_part = meta_ref[1] > 0
-    from_above = jnp.where(odd_part, fb_ref[...], fa_ref[...])
-    from_below = jnp.where(odd_part, fa_ref[...], fb_ref[...])
+    odd_part = lax.axis_index("dom") % 2 > 0
+    from_above = jnp.where(odd_part, fb_ref[:FACE], fa_ref[:FACE])
+    from_below = jnp.where(odd_part, fa_ref[:FACE], fb_ref[:FACE])
     near = weights[ITERS - 1] * jnp.where(lower, from_above, from_below)
     for m in range(ITERS - 1):
         near = near + weights[m] * near_ref[m]
@@ -466,10 +472,10 @@
                 high_mean = 0.5 * (highs[n] + up)
                 low_mean = 0.5 * (lows[n] + down)
                 if n == count - 1:
-                    edge = jnp.logical_and(jnp.logical_not(lower), meta_ref[3] > 0)
+                    edge = jnp.logical_and(jnp.logical_not(lower), part == parts - 1)
                     high_mean = jnp.where(edge, highs[n], high_mean)
                 if n == 0:
-                    edge = jnp.logical_and(lower, meta_ref[2] > 0)
+                    edge = jnp.logical_and(lower, part == 0)
                     low_mean = jnp.where(edge, lows[n], low_mean)
                 work[n, last, :] = high_mean
                 work[n, first, :] = low_mean
@@ -530,38 +536,50 @@
                 total = total + strain[a][c] * strain[c][b] + spin[a][c] * spin[c][b]
             mat[a][b] = total
             mat[b][a] = total
+    peak = jnp.maximum(jnp.abs(mat[0][1]), jnp.maximum(jnp.abs(mat[0][2]), jnp.abs(mat[1][2])))
+    for a in range(3):
+        peak = jnp.maximum(peak, jnp.abs(mat[a][a]))
+    peak = jnp.where(peak > 0.0, peak, 1.0)
+    shrink = 1.0 / peak
+    for a in range(3):
+        for b in range(a, 3):
+            mat[a][b] = mat[b][a] = mat[a][b] * shrink
     for _ in range(SWEEPS):
         for p, q, r in ((0, 1, 2), (0, 2, 1), (1, 2, 0)):
             pivot = mat[p][q]
             first, second = mat[p][p], mat[q][q]
-            num = 2.0 * pivot
-            den = first - second
-            size = jnp.maximum(jnp.abs(num), jnp.abs(den))
-            safe = jnp.where(size > 0.0, size, 1.0)
-            num_s = num / safe
-            den_s = den / safe
-            inv_norm = lax.rsqrt(jnp.where(size > 0.0, num_s * num_s + den_s * den_s, 1.0))
-            cos_two = jnp.where(size > 0.0, den_s * inv_norm, 1.0)
-            sin_two = num_s * inv_norm
-            big = jnp.sqrt(0.5 + 0.5 * jnp.abs(cos_two))
-            small = 0.5 * sin_two / big
+            gap = 0.5 * (first - second)
+            norm = pivot * pivot + gap * gap
+            inv_norm = lax.rsqrt(jnp.maximum(norm, 1e-37))
+            middle = 0.5 * (first + second)
+            radius = norm * inv_norm
+            turned = norm > 0.0
+            cos_two = jnp.where(turned, gap * inv_norm, 1.0)
+            half_sin = (0.5 * pivot) * inv_norm
+            lead = 0.5 + 0.5 * jnp.abs(cos_two)
+            inv_big = lax.rsqrt(lead)
+            big = lead * inv_big
+            small = half_sin * inv_big
             forward = cos_two >= 0.0
-            sign = jnp.where(num < 0.0, -1.0, 1.0)
             cosine = jnp.where(forward, big, jnp.abs(small))
-            sine = jnp.where(forward, small, sign * big)
-            cross = 2.0 * cosine * sine * pivot
-            cc, ss = cosine * cosine, sine * sine
+            sine = jnp.where(forward, small, jnp.where(pivot < 0.0, -big, big))
+            mat[p][p] = middle + radius
+            mat[q][q] = middle - radius
+            mat[p][q] = mat[q][p] = None
             side_p, side_q = mat[r][p], mat[r][q]
-            mat[p][p] = cc * first + cross + ss * second
-            mat[q][q] = ss * first - cross + cc * second
-            zero = jnp.zeros_like(pivot)
-            mat[p][q] = mat[q][p] = zero
-            mat[r][p] = mat[p][r] = cosine * side_p + sine * side_q
-            mat[r][q] = mat[q][r] = cosine * side_q - sine * side_p
+            if side_p is None:
+                new_p, new_q = sine * side_q, cosine * side_q
+            elif side_q is None:
+                new_p, new_q = cosine * side_p, -(sine * side_p)
+            else:
+                new_p = cosine * side_p + sine * side_q
+                new_q = cosine * side_q - sine * side_p
+            mat[r][p] = mat[p][r] = new_p
+            mat[r][q] = mat[q][r] = new_q
     d0, d1, d2 = mat[0][0], mat[1][1], mat[2][2]
     largest = jnp.maximum(jnp.maximum(d0, d1), d2)
     smallest = jnp.minimum(jnp.minimum(d0, d1), d2)
-    return d0 + d1 + d2 - largest - smallest
+    return (d0 + d1 + d2 - largest - smallest) * peak
 
 
 def vortex_kernel(grad_ref, place_ref, out_ref, value):
@@ -577,29 +595,33 @@
     high, mid, low = split3(value[...])
     place = place_ref[...]
     moved = dot_nt(place, high) + dot_nt(place, mid) + dot_nt(place, low)
-    out_ref[...] = moved.reshape(out_ref.shape)
-
-
-def final_kernel(meta_ref, vortex_ref, vel_ref, out_ref):
+    owners, cap = out_ref.shape[0], out_ref.shape[1]
+    used = place.shape[0] // cap
+    out_ref[: owners - used] = jnp.zeros((owners - used,) + out_ref.shape[1:], F32)
+    out_ref[owners - used :] = moved.reshape((used,) + out_ref.shape[1:])
+
+
+def final_kernel(vortex_ref, vel_ref, out_ref):
     quarters = vortex_ref.shape[0]
     quarter = vortex_ref.shape[2]
 
-    @pl.when(meta_ref[4] > 0)
+    last = lax.axis_index("grp") == lax.axis_size("grp") - 1
+
+    @pl.when(last)
     def _():
         for q in range(quarters):
             out_ref[0, :, q * quarter : (q + 1) * quarter] = vortex_ref[q]
 
-    @pl.when(meta_ref[4] == 0)
+    @pl.when(jnp.logical_not(last))
     def _():
         out_ref[0] = vel_ref[...]
 
 
+GRANT = pltpu.CompilerParams(vmem_limit_bytes=24 * 2**20)
+
+
 def vmem():
     return pl.BlockSpec(memory_space=pltpu.VMEM)
-
-
-def smem():
-    return pl.BlockSpec(memory_space=pltpu.SMEM)
 
 
 def cost(flops, size):
@@ -611,45 +633,24 @@
     nodes = forcing.shape[2]
     parts = lax.axis_size("dom")
     groups = lax.axis_size("grp")
-    part = lax.axis_index("dom")
-    group = lax.axis_index("grp")
     cap = elems // parts
     quarter = nodes // groups
     diff, kmat_np, cols_np, dcol_np, bound = host_tables()
     kmat = jnp.asarray(kmat_np, BF16)
     cols = jnp.asarray(cols_np)
     dcol = jnp.asarray(dcol_np)
-    meta = jnp.stack(
-        [
-            jnp.minimum(group, 2),
-            part % 2,
-            (part == 0).astype(jnp.int32),
-            (part == parts - 1).astype(jnp.int32),
-            (group == groups - 1).astype(jnp.int32),
-        ]
-    ).astype(jnp.int32)
-    coef = jnp.concatenate(
-        [viscosity[None], mass_coef[None], jnp.zeros((6, elems), F32)], axis=0
-    )
     sds = jax.ShapeDtypeStruct
 
     pack = pl.pallas_call(
         prep_kernel,
-        grid_spec=pltpu.PrefetchScalarGridSpec(
-            num_scalar_prefetch=1,
-            grid=(1,),
-            in_specs=[
-                pl.BlockSpec((1, elems, nodes), lambda n, m: (m[0], 0, 0)),
-                pl.BlockSpec((1, elems), lambda n, m: (0, 0)),
-                pl.BlockSpec((8, elems), lambda n, m: (0, 0)),
-                pl.BlockSpec((2, nodes, TILE), lambda n, m: (0, 0, 0)),
-            ],
-            out_specs=pl.BlockSpec((nodes + 8, elems), lambda n, m: (0, 0)),
-        ),
+        in_specs=[pl.BlockSpec(memory_space=pl.ANY)] + [vmem()] * 4,
+        out_specs=vmem(),
         out_shape=sds((nodes + 8, elems), F32),
+        scratch_shapes=[pltpu.VMEM((elems, nodes), F32), pltpu.SemaphoreType.DMA],
         cost_estimate=cost(10**9, 2 * 10**6),
+        compiler_params=GRANT,
         name="prep",
-    )(meta, forcing, element_order, coef, cols)
+    )(forcing, element_order, viscosity[None], mass_coef[None], cols)
 
     swap_a = [(i, i ^ 1) for i in range(parts) if i ^ 1 < parts]
     swap_b = [(i, ((i - 1) ^ 1) + 1) for i in range(1, parts - 1)]
@@ -662,18 +663,18 @@
         out_specs=vmem(),
         out_shape=sds((elems, elems), BF16),
         cost_estimate=cost(10**9, 2 * 10**6),
+        compiler_params=GRANT,
         name="place",
     )(element_order, owner)
 
-    basis, near, face, dots = pl.pallas_call(
+    basis, near, message = pl.pallas_call(
         lambda *refs: krylov_kernel(diff, bound, *refs),
-        in_specs=[smem()] + [vmem()] * 5,
-        out_specs=[vmem()] * 4,
+        in_specs=[vmem()] * 5,
+        out_specs=[vmem()] * 3,
         out_shape=[
             sds((ITERS, nodes, elems), F32),
             sds((ITERS - 1, FACE, TILE), F32),
-            sds((FACE, TILE), F32),
-            sds((16, 8, TILE), F32),
+            sds((FACE + 16, TILE), F32),
         ],
         scratch_shapes=[
             pltpu.VMEM((6, nodes, TILE), F32),
@@ -681,32 +682,35 @@
             pltpu.VMEM((6, nodes, TILE), F32),
             pltpu.VMEM((nodes, elems), F32),
             pltpu.VMEM((ITERS - 1, nodes, elems), F32),
-            pltpu.VMEM((3, nodes // 2, elems), BF16),
-            pltpu.VMEM((3, nodes // 2, elems), BF16),
+            pltpu.VMEM((2, nodes // 2, elems), BF16),
+            pltpu.VMEM((2, nodes // 2, elems), BF16),
             pltpu.VMEM((2, nodes // 2, elems), F32),
+            pltpu.VMEM((16, 8, TILE), F32),
         ],
         cost_estimate=cost(10**10, 10**7),
+        compiler_params=GRANT,
         name="krylov",
-    )(meta, pack, ghost_a, ghost_b, kmat, cols)
-
-    message = jnp.concatenate([face, jnp.sum(dots, axis=1)], axis=0)
+    )(pack, ghost_a, ghost_b, kmat, cols)
+
     face_a = lax.ppermute(message, "dom", swap_a)
-    face_b = lax.ppermute(face, "dom", swap_b)
-    sums = message[FACE:] + face_a[FACE:]
+    face_b = lax.ppermute(message, "dom", swap_b)
+    pending = (message[FACE:], face_a[FACE:])
     reach = 2
     while reach < parts:
-        sums = sums + lax.ppermute(sums, "dom", [(i, i ^ reach) for i in range(parts)])
+        sums = pending[0] + pending[1]
+        pending = (sums, lax.ppermute(sums, "dom", [(i, i ^ reach) for i in range(parts)]))
         reach *= 2
 
     grads, vel = pl.pallas_call(
         lambda *refs: gradient_kernel(diff, *refs),
-        in_specs=[smem()] + [vmem()] * 6,
+        in_specs=[vmem()] * 7,
         out_specs=[vmem()] * 2,
         out_shape=[sds((groups, 3, quarter, elems), BF16), sds((nodes, elems), F32)],
         scratch_shapes=[pltpu.VMEM((2, nodes, TILE), F32)],
         cost_estimate=cost(10**9, 4 * 10**6),
+        compiler_params=GRANT,
         name="gradient",
-    )(meta, sums, basis, near, face_a[:FACE], face_b, dcol)
+    )(*pending, basis, near, face_a, face_b, dcol)
 
     exchanged = lax.all_to_all(grads, "grp", split_axis=0, concat_axis=0, tiled=True)
 
@@ -716,6 +720,7 @@
         out_specs=vmem(),
         out_shape=sds((elems, nodes), F32),
         cost_estimate=cost(10**9, 2 * 10**6),
+        compiler_params=GRANT,
         name="slots",
     )(element_order, vel)
 
@@ -723,28 +728,25 @@
         vortex_kernel,
         in_specs=[vmem(), vmem()],
         out_specs=vmem(),
-        out_shape=sds((parts, cap, quarter), F32),
+        out_shape=sds((groups * parts, cap, quarter), F32),
         scratch_shapes=[pltpu.VMEM((quarter, elems), F32)],
         cost_estimate=cost(10**9, 2 * 10**6),
+        compiler_params=GRANT,
         name="vortex",
     )(exchanged, place)
 
-    padding = jnp.zeros(((groups - 1) * parts, cap, quarter), F32)
     received = lax.all_to_all(
-        jnp.concatenate([padding, packed], 0),
-        ("grp", "dom"),
-        split_axis=0,
-        concat_axis=0,
-        tiled=True,
+        packed, ("grp", "dom"), split_axis=0, concat_axis=0, tiled=True
     )
     return pl.pallas_call(
         final_kernel,
-        in_specs=[smem(), vmem(), vmem()],
+        in_specs=[vmem(), vmem()],
         out_specs=vmem(),
         out_shape=sds((1, elems, nodes), F32),
         cost_estimate=cost(10**6, 2 * 10**6),
+        compiler_params=GRANT,
         name="final",
-    )(meta, received.reshape(groups, elems, quarter), vel_slot)
+    )(received.reshape(groups, elems, quarter), vel_slot)
 
 
 def solution(mesh):

time: 99.4 us -> 81.9 us (0.82)
  Pallas kernels: 36.6 us -> 20.8 us
  other arithmetic: 3.59 us -> 0.01 us
  waiting for transfers between devices: 27.3 us -> 30.7 us
  local copies, waits for them, and re-layouts: 6.95 us -> 4.51 us
  starting transfers between devices: 24.4 us -> 25.4 us
    pallas_call x3, Pallas kernels: 10.2 us -> 4.87 us  [the longest x1 3.3 us: per_device(): pl.pallas_call(lambda *refs: gradient_kernel(diff, *refs), in_specs=[vmem...]
    pallas_call x1, Pallas kernels: 14.9 us -> 11.1 us  [per_device(): pl.pallas_call(lambda *refs: krylov_kernel(diff, bound, *refs), in_specs=...]
    pallas_call x1, Pallas kernels: 7.45 us -> 4.03 us  [per_device(): pl.pallas_call(vortex_kernel, in_specs=[vmem(), vmem()], out_specs=vmem()...]
    concatenate x2 -> x0, other arithmetic: 2.12 us -> none  [the longest x1 1.36 us: per_device(): jnp.concatenate([viscosity[None], mass_coef[None], jnp.zeros((6, elems),...]
    pallas_call x1, Pallas kernels: 2.29 us -> 0.44 us  [per_device(): pl.pallas_call(slots_kernel, in_specs=[vmem(), vmem()], out_specs=vmem(),...]
    all_to_all x1, waiting for transfers between devices: 13.9 us -> 15.8 us  [per_device(): lax.all_to_all(packed, ('grp', 'dom'), split_axis=0, concat_axis=0, tiled...]
    concatenate x2 -> x0, local copies, waits for them, and re-layouts: 1.84 us -> none  [the longest x1 1.76 us: per_device(): jnp.concatenate([padding, packed], 0)]
    all_to_all x1, waiting for transfers between devices: 8.68 us -> 10.1 us  [per_device(): lax.all_to_all(grads, 'grp', split_axis=0, concat_axis=0, tiled=True)]
  transfers between devices with their start and end apart: 8 -> 8, of which waited for: 6 -> 6; matrix products, arithmetic and copies ran while one was open for 1% -> 0% of each run, Pallas kernels for 4% -> 1%
where the time goes in v1:
time: 81.9 us; the launch traced here: 81.5 us
  waiting for transfers between devices  30.7 us (37%)
  starting transfers between devices  25.4 us (31%)
  Pallas kernels  20.8 us (25%)
  local copies, waits for them, and re-layouts  4.51 us (6%)
    all_to_all x1, waiting for transfers between devices, per_device(): lax.all_to_all(packed, ('grp', 'dom'), split_axis=0, concat_axis=0, tiled...  15.8 us
    pallas_call x1, Pallas kernels, per_device(): pl.pallas_call(lambda *refs: krylov_kernel(diff, bound, *refs), in_specs=...  11.1 us
    all_to_all x1, waiting for transfers between devices, per_device(): lax.all_to_all(grads, 'grp', split_axis=0, concat_axis=0, tiled=True)  10.1 us
    ppermute x1, starting transfers between devices, per_device(): face_a = lax.ppermute(message, 'dom', swap_a)  10 us
    ppermute x2, starting transfers between devices, per_device(): lax.ppermute(sums, 'dom', [(i, i ^ reach) for i in range(parts)])  6.01 us
    unnamed x20, local copies, waits for them, and re-layouts  4.51 us
    pallas_call x1, Pallas kernels, per_device(): pl.pallas_call(vortex_kernel, in_specs=[vmem(), vmem()], out_specs=vmem()...  4.03 us
    all_to_all x1, starting transfers between devices, per_device(): lax.all_to_all(grads, 'grp', split_axis=0, concat_axis=0, tiled=True)  3.79 us
  transfers between devices with their start and end apart: 8, of which 6 were waited for; matrix products, arithmetic and copies ran while one was open for 0% of the time, Pallas kernels for 1%

profile of v1, /device:TPU:0, one launch (start us, length us, event | category | flops | bytes accessed | tf_op | source)
XLA Modules:
  0.0 81.5 jit_solution(7895102561137843931)
XLA Ops:
  0.0 0.0 copy-start
  0.0 1.4 %copy-done = f32[3,256,512]{2,1,0:T(8,128)S(1)} copy-done((f32[3,256,512]{2,1,0:T(8,128)S(1)}, f32[3,256,512]{2,1,0:T(8,128)}, u32[]{:S(2)}) %copy-start) | copy-done | bytes 1572888
  1.4 0.0 copy-start.1
  1.4 0.7 copy-done.1
  2.1 0.0 copy-start.2
  2.1 0.7 copy-done.2
  2.8 0.0 copy-start.4
  2.8 0.7 copy-done.4
  3.4 0.0 copy-start.7
  3.4 1.0 %copy-done.7 = f32[2,512,128]{2,1,0:T(8,128)S(1)} copy-done((f32[2,512,128]{2,1,0:T(8,128)S(1)}, f32[2,512,128]{2,1,0:T(8,128)}, u32[]{:S(2)}) %copy-start.7) | copy-done | bytes 524312
  4.5 0.0 copy-start.6
  4.5 0.0 copy-start.8
  4.5 0.7 prep.1.refs_0_
  5.2 0.0 copy-start.9
  5.3 0.6 collective-permute-start
  5.8 0.7 collective-permute-start.1
  6.5 0.9 %collective-permute-done.refs_1_ = f32[520,256]{1,0:T(8,128)S(1)} collective-permute-done((f32[520,256]{1,0:T(8,128)S(1)}, f32[520,256]{1,0:T(8,128)S(1)}, u32[]{:S(2)}, u32[]{:S(2)}) %collective-permute-start) | collective-permute-done | bytes 532512 | tf_op jit(solution)/shard_map/ppermute | solution.py:657
  7.4 0.0 collective-permute-done.1.refs_2_
  7.4 0.0 copy-done.6
  7.4 0.0 copy-done.8
  7.4 11.1 %krylov.1 = (f32[4,512,256]{2,1,0:T(8,128)S(1)}, f32[3,64,128]{2,1,0:T(8,128)S(1)}, f32[80,128]{1,0:T(8,128)S(1)}) custom-call(f32[520,256]{1,0:T(8,128)S(1)} %prep.1.refs_0_, f32[520,256]{1,0:T(8,128)S(1)} %collective-permute-done.refs_1_, f32[520,256]{1,0:T(8,128)S(1)} %collective-permute-done.1.refs_2_, bf16[6,256,256]{2,1,0:T(8,128)(2,1)S(1)} %copy-done.6, ...), custom_call_target="tpu_custom_call" | custom-call | flops 10000000000 | bytes 10000000 | tf_op jit(solution)/shard_map/krylov/pallas_call | solution.py:670
  18.5 10.0 %collective-permute-start.2 = (f32[80,128]{1,0:T(8,128)S(1)}, f32[80,128]{1,0:T(8,128)S(1)}, u32[]{:S(2)}, u32[]{:S(2)}) collective-permute-start(f32[80,128]{1,0:T(8,128)S(1)} %get-tuple-element.10), channel_id=1, source_target_pairs={{0,1},{1,0},{2,3},{3,2},{4,5},{5,4},{6,7},{7,6},{8,9},{9,8},{10,11... | collective-permute-start | bytes 122888 | tf_op jit(solution)/shard_map/ppermute | solution.py:695
  28.6 0.7 collective-permute-start.5
  29.2 0.2 collective-permute-done.2.refs_4_
  29.4 3.2 %collective-permute-start.3 = (f32[16,128]{1,0:T(8,128)S(1)}, f32[16,128]{1,0:T(8,128)S(1)}, u32[]{:S(2)}, u32[]{:S(2)}) collective-permute-start(f32[16,128]{1,0:T(8,128)S(1)} %slice_add_fusion), channel_id=1, source_target_pairs={{0,2},{1,3},{2,0},{3,1},{4,6},{5,7},{6,4},{7,5},{8,10},{9,11},{10,... | collective-permute-start | bytes 24584 | tf_op jit(solution)/shard_map/ppermute | solution.py:701
  32.7 2.0 %collective-permute-done.3 = f32[16,128]{1,0:T(8,128)S(1)} collective-permute-done((f32[16,128]{1,0:T(8,128)S(1)}, f32[16,128]{1,0:T(8,128)S(1)}, u32[]{:S(2)}, u32[]{:S(2)}) %collective-permute-start.3) | collective-permute-done | bytes 8224 | tf_op jit(solution)/shard_map/ppermute | solution.py:701
  34.6 2.8 %collective-permute-start.4 = (f32[16,128]{1,0:T(8,128)S(1)}, f32[16,128]{1,0:T(8,128)S(1)}, u32[]{:S(2)}, u32[]{:S(2)}) collective-permute-start(f32[16,128]{1,0:T(8,128)S(1)} %add.7.refs_0_), channel_id=1, source_target_pairs={{0,4},{1,5},{2,6},{3,7},{4,0},{5,1},{6,2},{7,3},{8,12},{9,13},{10,... | collective-permute-start | bytes 24584 | tf_op jit(solution)/shard_map/ppermute | solution.py:701
  37.4 0.0 collective-permute-done.5.refs_5_
  37.4 1.8 %collective-permute-done.4.refs_1_ = f32[16,128]{1,0:T(8,128)S(1)} collective-permute-done((f32[16,128]{1,0:T(8,128)S(1)}, f32[16,128]{1,0:T(8,128)S(1)}, u32[]{:S(2)}, u32[]{:S(2)}) %collective-permute-start.4) | collective-permute-done | bytes 8224 | tf_op jit(solution)/shard_map/ppermute | solution.py:701
  39.2 0.0 copy-done.9
  39.2 0.0 copy-start.3
  39.2 0.0 copy-start.5
  39.2 3.3 %gradient.1 = (bf16[4,3,128,256]{3,2,1,0:T(8,128)(2,1)}, f32[512,256]{1,0:T(8,128)S(1)}) custom-call(f32[16,128]{1,0:T(8,128)S(1)} %add.7.refs_0_, f32[16,128]{1,0:T(8,128)S(1)} %collective-permute-done.4.refs_1_, f32[4,512,256]{2,1,0:T(8,128)S(1)} %get-tuple-element.11.refs_2_, f32[3,64,128]{2,1,0:T(8,128)S(1)} %get-tuple-element.12.refs_3_, ...), custom_call_target="tpu_custom_call" | custom-call | flops 1000000000 | bytes 4000000 | tf_op jit(solution)/shard_map/gradient/pallas_call | solution.py:704
  42.5 3.8 %all-to-all-start = ((bf16[4,3,128,256]{3,2,1,0:T(8,128)(2,1)}), bf16[4,3,128,256]{3,2,1,0:T(8,128)(2,1)S(1)}, u32[]{:S(2)}, u32[]{:S(2)}) async-start(bf16[4,3,128,256]{3,2,1,0:T(8,128)(2,1)} %get-tuple-element.13), calls=%async_computation | async-start | bytes 1572864 | tf_op jit(solution)/shard_map/all_to_all | solution.py:715
  46.3 0.0 copy-done.3
  46.3 0.0 copy-done.5
  46.3 0.3 place.1.place_ref
  46.6 10.1 %all-to-all-done.grad_ref = bf16[4,3,128,256]{3,2,1,0:T(8,128)(2,1)S(1)} async-done(((bf16[4,3,128,256]{3,2,1,0:T(8,128)(2,1)}), bf16[4,3,128,256]{3,2,1,0:T(8,128)(2,1)S(1)}, u32[]{:S(2)}, u32[]{:S(2)}) %all-to-all-start) | async-done | bytes 786464 | tf_op jit(solution)/shard_map/all_to_all | solution.py:715
  56.7 4.0 %vortex.1 = f32[32,32,128]{2,1,0:T(8,128)} custom-call(bf16[4,3,128,256]{3,2,1,0:T(8,128)(2,1)S(1)} %all-to-all-done.grad_ref, bf16[256,256]{1,0:T(8,128)(2,1)S(1)} %place.1.place_ref), custom_call_target="tpu_custom_call" | custom-call | flops 1000000000 | bytes 2000000 | tf_op jit(solution)/shard_map/vortex/pallas_call | solution.py:727
  60.8 3.7 %all-to-all-start.1 = ((f32[32,32,128]{2,1,0:T(8,128)}), f32[32,32,128]{2,1,0:T(8,128)S(1)}, u32[]{:S(2)}, u32[]{:S(2)}) async-start(f32[32,32,128]{2,1,0:T(8,128)} %vortex.1), calls=%async_computation.1 | async-start | bytes 1048576 | tf_op jit(solution)/shard_map/all_to_all | solution.py:738
  64.5 0.4 slots.1.vel_ref
  64.9 15.8 %all-to-all-done.1 = f32[32,32,128]{2,1,0:T(8,128)S(1)} async-done(((f32[32,32,128]{2,1,0:T(8,128)}), f32[32,32,128]{2,1,0:T(8,128)S(1)}, u32[]{:S(2)}, u32[]{:S(2)}) %all-to-all-start.1) | async-done | bytes 524320 | tf_op jit(solution)/shard_map/all_to_all | solution.py:738
  80.7 0.8 %final.1 = f32[1,256,512]{2,1,0:T(8,128)} custom-call(f32[4,256,128]{2,1,0:T(8,128)S(1)} %bitcast.3, f32[256,512]{1,0:T(8,128)S(1)} %slots.1.vel_ref), custom_call_target="tpu_custom_call" | custom-call | flops 1000000 | bytes 2000000 | tf_op jit(solution)/shard_map/final/pallas_call | solution.py:741
  (2 shorter events, 0.0 us)
Async XLA Ops:
  0.0 1.4 %copy-start = (f32[3,256,512]{2,1,0:T(8,128)S(1)}, f32[3,256,512]{2,1,0:T(8,128)}, u32[]{:S(2)}) copy-start(f32[3,256,512]{2,1,0:T(8,128)} %force_any.1) | copy-start | bytes 4718596
  1.4 0.7 copy-start.1
  2.1 0.7 copy-start.2
  2.8 0.7 copy-start.4
  3.4 1.0 %copy-start.7 = (f32[2,512,128]{2,1,0:T(8,128)S(1)}, f32[2,512,128]{2,1,0:T(8,128)}, u32[]{:S(2)}) copy-start(f32[2,512,128]{2,1,0:T(8,128)} %constant.7.clone.cols_ref.refs_4_) | copy-start | bytes 1572868
  4.5 2.9 %copy-start.6 = (bf16[6,256,256]{2,1,0:T(8,128)(2,1)S(1)}, bf16[6,256,256]{2,1,0:T(8,128)(2,1)}, u32[]{:S(2)}) copy-start(bf16[6,256,256]{2,1,0:T(8,128)(2,1)} %constant.6.clone.refs_3_) | copy-start | bytes 2359300
  4.5 2.9 %copy-start.8 = (f32[2,512,128]{2,1,0:T(8,128)S(1)}, f32[2,512,128]{2,1,0:T(8,128)}, u32[]{:S(2)}) copy-start(f32[2,512,128]{2,1,0:T(8,128)} %constant.7.clone.cols_ref.refs_4_) | copy-start | bytes 1572868
  5.2 33.9 %copy-start.9 = (f32[8,8,128]{2,1,0:T(8,128)S(1)}, f32[8,8,128]{2,1,0:T(8,128)}, u32[]{:S(2)}) copy-start(f32[8,8,128]{2,1,0:T(8,128)} %constant.8.clone.refs_6_) | copy-start | bytes 98308
  5.3 2.1 %collective-permute-start = (f32[520,256]{1,0:T(8,128)S(1)}, f32[520,256]{1,0:T(8,128)S(1)}, u32[]{:S(2)}, u32[]{:S(2)}) collective-permute-start(f32[520,256]{1,0:T(8,128)S(1)} %prep.1.refs_0_), channel_id=1, source_target_pairs={{0,1},{1,0},{2,3},{3,2},{4,5},{5,4},{6,7},{7,6},{8,9},{9,8},{10,11... | collective-permute-start | bytes 1597448 | tf_op jit(solution)/shard_map/ppermute | solution.py:657
  5.8 1.6 %collective-permute-start.1 = (f32[520,256]{1,0:T(8,128)S(1)}, f32[520,256]{1,0:T(8,128)S(1)}, u32[]{:S(2)}, u32[]{:S(2)}) collective-permute-start(f32[520,256]{1,0:T(8,128)S(1)} %prep.1.refs_0_), channel_id=1, source_target_pairs={{1,2},{2,1},{3,4},{4,3},{5,6},{6,5},{9,10},{10,9},{11,12},{12,11},... | collective-permute-start | bytes 1597448 | tf_op jit(solution)/shard_map/ppermute | solution.py:658
  18.5 10.9 %collective-permute-start.2 = (f32[80,128]{1,0:T(8,128)S(1)}, f32[80,128]{1,0:T(8,128)S(1)}, u32[]{:S(2)}, u32[]{:S(2)}) collective-permute-start(f32[80,128]{1,0:T(8,128)S(1)} %get-tuple-element.10), channel_id=1, source_target_pairs={{0,1},{1,0},{2,3},{3,2},{4,5},{5,4},{6,7},{7,6},{8,9},{9,8},{10,11... | collective-permute-start | bytes 122888 | tf_op jit(solution)/shard_map/ppermute | solution.py:695
  28.6 8.8 %collective-permute-start.5 = (f32[80,128]{1,0:T(8,128)S(1)}, f32[80,128]{1,0:T(8,128)S(1)}, u32[]{:S(2)}, u32[]{:S(2)}) collective-permute-start(f32[80,128]{1,0:T(8,128)S(1)} %get-tuple-element.10), channel_id=1, source_target_pairs={{1,2},{2,1},{3,4},{4,3},{5,6},{6,5},{9,10},{10,9},{11,12},{12,11},... | collective-permute-start | bytes 122888 | tf_op jit(solution)/shard_map/ppermute | solution.py:696
  29.4 5.2 %collective-permute-start.3 = (f32[16,128]{1,0:T(8,128)S(1)}, f32[16,128]{1,0:T(8,128)S(1)}, u32[]{:S(2)}, u32[]{:S(2)}) collective-permute-start(f32[16,128]{1,0:T(8,128)S(1)} %slice_add_fusion), channel_id=1, source_target_pairs={{0,2},{1,3},{2,0},{3,1},{4,6},{5,7},{6,4},{7,5},{8,10},{9,11},{10,... | collective-permute-start | bytes 24584 | tf_op jit(solution)/shard_map/ppermute | solution.py:701
  34.6 4.5 %collective-permute-start.4 = (f32[16,128]{1,0:T(8,128)S(1)}, f32[16,128]{1,0:T(8,128)S(1)}, u32[]{:S(2)}, u32[]{:S(2)}) collective-permute-start(f32[16,128]{1,0:T(8,128)S(1)} %add.7.refs_0_), channel_id=1, source_target_pairs={{0,4},{1,5},{2,6},{3,7},{4,0},{5,1},{6,2},{7,3},{8,12},{9,13},{10,... | collective-permute-start | bytes 24584 | tf_op jit(solution)/shard_map/ppermute | solution.py:701
  39.2 7.1 %copy-start.3 = (s32[1,256]{1,0:T(1,128)S(1)}, s32[1,256]{1,0:T(1,128)}, u32[]{:S(2)}) copy-start(s32[1,256]{1,0:T(1,128)} %refs_1_.1) | copy-start | bytes 3076
  39.2 7.1 %copy-start.5 = (s32[1,256]{1,0:T(1,128)S(1)}, s32[1,256]{1,0:T(1,128)}, u32[]{:S(2)}) copy-start(s32[1,256]{1,0:T(1,128)} %order_ref.3) | copy-start | bytes 3076
  42.5 14.2 %all-to-all-start = ((bf16[4,3,128,256]{3,2,1,0:T(8,128)(2,1)}), bf16[4,3,128,256]{3,2,1,0:T(8,128)(2,1)S(1)}, u32[]{:S(2)}, u32[]{:S(2)}) async-start(bf16[4,3,128,256]{3,2,1,0:T(8,128)(2,1)} %get-tuple-element.13), calls=%async_computation | async-start | bytes 1572864 | tf_op jit(solution)/shard_map/all_to_all | solution.py:715
  60.8 19.9 %all-to-all-start.1 = ((f32[32,32,128]{2,1,0:T(8,128)}), f32[32,32,128]{2,1,0:T(8,128)S(1)}, u32[]{:S(2)}, u32[]{:S(2)}) async-start(f32[32,32,128]{2,1,0:T(8,128)} %vortex.1), calls=%async_computation.1 | async-start | bytes 1048576 | tf_op jit(solution)/shard_map/all_to_all | solution.py:738

commit v2 on v1

--- a/solution.py
+++ b/solution.py
@@ -121,24 +121,39 @@
     return jnp.concatenate([col] * (lanes // col.shape[1]), axis=1)
 
 
-def prep_kernel(force_any, order_ref, visc_ref, mass_ref, cols_ref, pack_ref, force_ref, sem):
+def prep_kernel(
+    force_hbm, order_hbm, visc_hbm, mass_hbm, cols_hbm, pack_ref,
+    force_ref, order_ref, visc_ref, mass_ref, cols_ref, sem,
+):
     elems = order_ref.shape[1]
-    nodes = force_any.shape[2]
+    nodes = force_ref.shape[1]
     component = jnp.minimum(lax.axis_index("grp"), 2)
-    fetch = pltpu.make_async_copy(force_any.at[component], force_ref, sem)
-    fetch.start()
+    copies = [
+        pltpu.make_async_copy(order_hbm, order_ref, sem.at[0]),
+        pltpu.make_async_copy(visc_hbm, visc_ref, sem.at[1]),
+        pltpu.make_async_copy(mass_hbm, mass_ref, sem.at[2]),
+        pltpu.make_async_copy(force_hbm.at[component], force_ref, sem.at[3]),
+        pltpu.make_async_copy(cols_hbm.at[0], cols_ref, sem.at[4]),
+    ]
+    for copy in copies:
+        copy.start()
+    for copy in copies[:3]:
+        copy.wait()
     cell_by_slot = (iota((elems, elems), 0) == order_ref[...]).astype(F32)
     perm = jnp.transpose(cell_by_slot).astype(BF16)
     coef = jnp.concatenate([visc_ref[...], mass_ref[...], jnp.zeros((6, elems), F32)], axis=0)
     high, mid, low = split3(coef)
-    pack_ref[nodes:, :] = dot_nn(high, perm) + dot_nn(mid, perm) + dot_nn(low, perm)
-    fetch.wait()
+    coef = dot_nn(high, perm) + dot_nn(mid, perm) + dot_nn(low, perm)
+    pack_ref[nodes:, :] = coef
+    for copy in copies[3:]:
+        copy.wait()
     chunk = 128
     for at in range(0, nodes, chunk):
         piece = jnp.transpose(force_ref[:, at : at + chunk])
         high, mid, low = split3(piece)
         moved = dot_nn(high, perm) + dot_nn(mid, perm) + dot_nn(low, perm)
-        pack_ref[at : at + chunk, :] = wide(cols_ref[0, at : at + chunk, :], elems) * moved
+        moved = wide(cols_ref[at : at + chunk, :], elems) * moved
+        pack_ref[at : at + chunk, :] = moved
 
 
 def place_kernel(cap, order_ref, owner_ref, place_ref):
@@ -215,8 +230,29 @@
         ref[t, first, :] = lows[n] + down
 
 
+def stage_kernel(own_ref, cols_ref, raw_ref, rhs_ref, jac_ref):
+    nodes = cols_ref.shape[1]
+    elems = own_ref.shape[1]
+    raw_ref[nodes:, :] = own_ref[nodes:, :]
+
+    @pl.loop(0, NP)
+    def _(k):
+        rows = pl.ds(pl.multiple_of(k * FACE, FACE), FACE)
+        value = own_ref[rows, :]
+        raw_ref[rows, :] = value
+        save_block(rhs_ref, 0, rows, value)
+        w_col = wide(cols_ref[0, rows, :], elems)
+        d_col = wide(cols_ref[1, rows, :], elems)
+        visc = own_ref[nodes : nodes + 1, :]
+        mass = own_ref[nodes + 1 : nodes + 2, :]
+        save_block(jac_ref, 0, rows, visc * d_col + mass * w_col)
+
+    share_xy(rhs_ref, [0, 1])
+    share_xy(jac_ref, [0, 1])
+
+
 def krylov_kernel(
-    diff, bound, own_ref, a_ref, b_ref, kmat_ref, cols_ref,
+    diff, bound, own_ref, rhs_ref, jac_ref, a_ref, b_ref, kmat_ref, cols_ref,
     basis_ref, near_ref, message_ref,
     work, coef, inv, vec, ghost, even, odd, prod, dots_ref,
 ):
@@ -228,8 +264,7 @@
     wide_tile = pl.ds(0, TILE)
     high_tile = pl.ds(TILE, TILE)
 
-    def gather(rows, out_own, out_near, out_far):
-        out_own(own_ref[rows, :])
+    def gather(rows, out_near, out_far):
         a_low, a_high = a_ref[rows, wide_tile], a_ref[rows, high_tile]
         b_low, b_high = b_ref[rows, wide_tile], b_ref[rows, high_tile]
         out_near(
@@ -250,22 +285,26 @@
         return put
 
     tail = pl.ds(nodes, own_ref.shape[0] - nodes)
-    gather(tail, store_coef(0), store_coef(1), store_coef(2))
+    coef[0] = own_ref[tail, :]
+    gather(tail, store_coef(1), store_coef(2))
 
     @pl.loop(0, NP)
     def _(k):
         rows = pl.ds(pl.multiple_of(k * FACE, FACE), FACE)
-        gather(rows, store(work, 0, rows), store(work, 1, rows), store(work, 2, rows))
+        gather(rows, store(work, 1, rows), store(work, 2, rows))
+        for t in range(2):
+            work[t, rows, :] = rhs_ref[t, rows, :]
+            inv[t, rows, :] = jac_ref[t, rows, :]
         w_col = wide(cols_ref[0, rows, :], elems)
         d_col = wide(cols_ref[1, rows, :], elems)
-        for n in range(3):
+        for n in range(1, 3):
             save_block(inv, n, rows, coef[n, 0:1, :] * d_col + coef[n, 1:2, :] * w_col)
 
     far_tiles = [4, 2, 0, 1, 3, 5]
     near_tiles = far_tiles[1:5]
-    share_xy(work, far_tiles)
+    share_xy(work, [2, 3, 4, 5])
     share_z(work, far_tiles)
-    share_xy(inv, far_tiles)
+    share_xy(inv, [2, 3, 4, 5])
     share_z(inv, far_tiles)
 
     @pl.loop(0, NP)
@@ -617,6 +656,7 @@
         out_ref[0] = vel_ref[...]
 
 
+PREP_LIMIT = 67043328 - 2600 * 1024
 GRANT = pltpu.CompilerParams(vmem_limit_bytes=24 * 2**20)
 
 
@@ -643,19 +683,40 @@
 
     pack = pl.pallas_call(
         prep_kernel,
-        in_specs=[pl.BlockSpec(memory_space=pl.ANY)] + [vmem()] * 4,
+        in_specs=[pl.BlockSpec(memory_space=pltpu.HBM)] * 5,
         out_specs=vmem(),
         out_shape=sds((nodes + 8, elems), F32),
-        scratch_shapes=[pltpu.VMEM((elems, nodes), F32), pltpu.SemaphoreType.DMA],
+        scratch_shapes=[
+            pltpu.VMEM((elems, nodes), F32),
+            pltpu.VMEM((1, elems), jnp.int32),
+            pltpu.VMEM((1, elems), F32),
+            pltpu.VMEM((1, elems), F32),
+            pltpu.VMEM((nodes, TILE), F32),
+            pltpu.SemaphoreType.DMA((5,)),
+        ],
+        cost_estimate=cost(10**9, 2 * 10**6),
+        compiler_params=pltpu.CompilerParams(vmem_limit_bytes=PREP_LIMIT),
+        name="prep",
+    )(forcing, element_order, viscosity[None], mass_coef[None], cols)
+
+    swap_a = [(i, i ^ 1) for i in range(parts) if i ^ 1 < parts]
+    swap_b = [(i, ((i - 1) ^ 1) + 1) for i in range(1, parts - 1)]
+    ghost_b = lax.ppermute(pack, "dom", swap_b)
+    ghost_a = lax.ppermute(pack, "dom", swap_a)
+
+    raw, rhs_xy, jac_xy = pl.pallas_call(
+        stage_kernel,
+        in_specs=[vmem()] * 2,
+        out_specs=[vmem()] * 3,
+        out_shape=[
+            sds((nodes + 8, elems), F32),
+            sds((2, nodes, TILE), F32),
+            sds((2, nodes, TILE), F32),
+        ],
         cost_estimate=cost(10**9, 2 * 10**6),
         compiler_params=GRANT,
-        name="prep",
-    )(forcing, element_order, viscosity[None], mass_coef[None], cols)
-
-    swap_a = [(i, i ^ 1) for i in range(parts) if i ^ 1 < parts]
-    swap_b = [(i, ((i - 1) ^ 1) + 1) for i in range(1, parts - 1)]
-    ghost_a = lax.ppermute(pack, "dom", swap_a)
-    ghost_b = lax.ppermute(pack, "dom", swap_b)
+        name="stage",
+    )(pack, cols)
 
     place = pl.pallas_call(
         lambda *refs: place_kernel(cap, *refs),
@@ -669,7 +730,7 @@
 
     basis, near, message = pl.pallas_call(
         lambda *refs: krylov_kernel(diff, bound, *refs),
-        in_specs=[vmem()] * 5,
+        in_specs=[vmem()] * 7,
         out_specs=[vmem()] * 3,
         out_shape=[
             sds((ITERS, nodes, elems), F32),
@@ -690,7 +751,7 @@
         cost_estimate=cost(10**10, 10**7),
         compiler_params=GRANT,
         name="krylov",
-    )(pack, ghost_a, ghost_b, kmat, cols)
+    )(raw, rhs_xy, jac_xy, ghost_a, ghost_b, kmat, cols)
 
     face_a = lax.ppermute(message, "dom", swap_a)
     face_b = lax.ppermute(message, "dom", swap_b)

time: 81.9 us -> 78.9 us (0.963)
  local copies, waits for them, and re-layouts: 4.51 us -> 1.06 us
  Pallas kernels: 20.8 us -> 22.6 us
  waiting for transfers between devices: 30.7 us -> 29.8 us
    unnamed x20 -> x12, local copies, waits for them, and re-layouts: 4.51 us -> 1.06 us
    pallas_call x1 -> x2, Pallas kernels: 0.75 us -> 2.95 us  [the longest x1 2.54 us: per_device(): pl.pallas_call(prep_kernel, in_specs=[pl.BlockSpec(memory_space=pltpu.HBM...]
    ppermute x1, waiting for transfers between devices: 0.86 us -> 0.01 us  [per_device(): ghost_a = lax.ppermute(pack, 'dom', swap_a)]
  transfers between devices with their start and end apart: 8 -> 8, of which waited for: 6 -> 5; matrix products, arithmetic and copies ran while one was open for 0% -> 0% of each run, Pallas kernels for 1% -> 2%
where the time goes in v2:
time: 78.9 us; the launch traced here: 78.6 us
  waiting for transfers between devices  29.8 us (38%)
  starting transfers between devices  25 us (32%)
  Pallas kernels  22.6 us (29%)
  local copies, waits for them, and re-layouts  1.06 us (1%)
    all_to_all x1, waiting for transfers between devices, per_device(): lax.all_to_all(packed, ('grp', 'dom'), split_axis=0, concat_axis=0, tiled...  15.8 us
    pallas_call x1, Pallas kernels, per_device(): pl.pallas_call(lambda *refs: krylov_kernel(diff, bound, *refs), in_specs=...  10.7 us
    all_to_all x1, waiting for transfers between devices, per_device(): lax.all_to_all(grads, 'grp', split_axis=0, concat_axis=0, tiled=True)  10.1 us
    ppermute x1, starting transfers between devices, per_device(): face_a = lax.ppermute(message, 'dom', swap_a)  9.61 us
    ppermute x2, starting transfers between devices, per_device(): lax.ppermute(sums, 'dom', [(i, i ^ reach) for i in range(parts)])  6.01 us
    pallas_call x1, Pallas kernels, per_device(): pl.pallas_call(vortex_kernel, in_specs=[vmem(), vmem()], out_specs=vmem()...  4.03 us
    all_to_all x1, starting transfers between devices, per_device(): lax.all_to_all(grads, 'grp', split_axis=0, concat_axis=0, tiled=True)  3.78 us
    ppermute x2, waiting for transfers between devices, per_device(): lax.ppermute(sums, 'dom', [(i, i ^ reach) for i in range(parts)])  3.72 us
  transfers between devices with their start and end apart: 8, of which 5 were waited for; matrix products, arithmetic and copies ran while one was open for 0% of the time, Pallas kernels for 2%

profile of v2, /device:TPU:0, one launch (start us, length us, event | category | flops | bytes accessed | tf_op | source)
XLA Modules:
  0.0 78.6 jit_solution(12878694291272552378)
XLA Ops:
  0.0 0.0 copy-start.4
  0.0 0.0 copy-start.3
  0.0 2.5 %prep.1.own_ref = f32[520,256]{1,0:T(8,128)} custom-call(f32[3,256,512]{2,1,0:T(8,128)} %force_hbm.1, s32[1,256]{1,0:T(1,128)} %order_ref.1, f32[1,256]{1,0:T(1,128)} %bitcast.4, f32[1,256]{1,0:T(1,128)} %bitcast.5, f32[2,512,128]{2,1,0:T(8,128)} %constant.7.clone.cols_hbm.cols_ref.refs_6_), custom_call_target="tpu_custom_call" | custom-call | flops 1000000000 | bytes 2000000 | tf_op jit(solution)/shard_map/prep/pallas_call | solution.py:684
  2.5 0.6 collective-permute-start
  3.1 0.7 collective-permute-start.1
  3.8 0.0 copy-done.4
  3.8 0.0 copy-start
  3.8 1.0 %copy-done = f32[520,256]{1,0:T(8,128)S(1)} copy-done((f32[520,256]{1,0:T(8,128)S(1)}, f32[520,256]{1,0:T(8,128)}, u32[]{:S(2)}) %copy-start) | copy-done | bytes 532504
  4.9 0.4 stage.1
  5.3 0.0 collective-permute-done.refs_3_
  5.3 0.0 collective-permute-done.1.refs_4_
  5.3 0.0 copy-done.3
  5.3 0.0 copy-start.5
  5.3 10.7 %krylov.1 = (f32[4,512,256]{2,1,0:T(8,128)S(1)}, f32[3,64,128]{2,1,0:T(8,128)S(1)}, f32[80,128]{1,0:T(8,128)S(1)}) custom-call(f32[520,256]{1,0:T(8,128)S(1)} %get-tuple-element.13.refs_0_, f32[2,512,128]{2,1,0:T(8,128)S(1)} %get-tuple-element.14.refs_1_, f32[2,512,128]{2,1,0:T(8,128)S(1)} %get-tuple-element.15.refs_2_, ...), custom_call_target="tpu_custom_call" | custom-call | flops 10000000000 | bytes 10000000 | tf_op jit(solution)/shard_map/krylov/pallas_call | solution.py:731
  16.0 9.6 %collective-permute-start.2 = (f32[80,128]{1,0:T(8,128)S(1)}, f32[80,128]{1,0:T(8,128)S(1)}, u32[]{:S(2)}, u32[]{:S(2)}) collective-permute-start(f32[80,128]{1,0:T(8,128)S(1)} %get-tuple-element.16), channel_id=1, source_target_pairs={{0,1},{1,0},{2,3},{3,2},{4,5},{5,4},{6,7},{7,6},{8,9},{9,8},{10,11... | collective-permute-start | bytes 122888 | tf_op jit(solution)/shard_map/ppermute | solution.py:756
  25.6 0.7 collective-permute-start.5
  26.3 0.2 collective-permute-done.2.refs_4_
  26.5 3.2 %collective-permute-start.3 = (f32[16,128]{1,0:T(8,128)S(1)}, f32[16,128]{1,0:T(8,128)S(1)}, u32[]{:S(2)}, u32[]{:S(2)}) collective-permute-start(f32[16,128]{1,0:T(8,128)S(1)} %slice_add_fusion), channel_id=1, source_target_pairs={{0,2},{1,3},{2,0},{3,1},{4,6},{5,7},{6,4},{7,5},{8,10},{9,11},{10,... | collective-permute-start | bytes 24584 | tf_op jit(solution)/shard_map/ppermute | solution.py:762
  29.7 2.0 %collective-permute-done.3 = f32[16,128]{1,0:T(8,128)S(1)} collective-permute-done((f32[16,128]{1,0:T(8,128)S(1)}, f32[16,128]{1,0:T(8,128)S(1)}, u32[]{:S(2)}, u32[]{:S(2)}) %collective-permute-start.3) | collective-permute-done | bytes 8224 | tf_op jit(solution)/shard_map/ppermute | solution.py:762
  31.7 2.8 %collective-permute-start.4 = (f32[16,128]{1,0:T(8,128)S(1)}, f32[16,128]{1,0:T(8,128)S(1)}, u32[]{:S(2)}, u32[]{:S(2)}) collective-permute-start(f32[16,128]{1,0:T(8,128)S(1)} %add.7.refs_0_), channel_id=1, source_target_pairs={{0,4},{1,5},{2,6},{3,7},{4,0},{5,1},{6,2},{7,3},{8,12},{9,13},{10,... | collective-permute-start | bytes 24584 | tf_op jit(solution)/shard_map/ppermute | solution.py:762
  34.5 0.0 collective-permute-done.5.refs_5_
  34.5 1.8 %collective-permute-done.4.refs_1_ = f32[16,128]{1,0:T(8,128)S(1)} collective-permute-done((f32[16,128]{1,0:T(8,128)S(1)}, f32[16,128]{1,0:T(8,128)S(1)}, u32[]{:S(2)}, u32[]{:S(2)}) %collective-permute-start.4) | collective-permute-done | bytes 8224 | tf_op jit(solution)/shard_map/ppermute | solution.py:762
  36.2 0.0 copy-done.5
  36.2 0.0 copy-start.1
  36.2 0.0 copy-start.2
  36.2 3.3 %gradient.1 = (bf16[4,3,128,256]{3,2,1,0:T(8,128)(2,1)}, f32[512,256]{1,0:T(8,128)S(1)}) custom-call(f32[16,128]{1,0:T(8,128)S(1)} %add.7.refs_0_, f32[16,128]{1,0:T(8,128)S(1)} %collective-permute-done.4.refs_1_, f32[4,512,256]{2,1,0:T(8,128)S(1)} %get-tuple-element.17.refs_2_, f32[3,64,128]{2,1,0:T(8,128)S(1)} %get-tuple-element.18.refs_3_, ...), custom_call_target="tpu_custom_call" | custom-call | flops 1000000000 | bytes 4000000 | tf_op jit(solution)/shard_map/gradient/pallas_call | solution.py:765
  39.5 3.8 %all-to-all-start = ((bf16[4,3,128,256]{3,2,1,0:T(8,128)(2,1)}), bf16[4,3,128,256]{3,2,1,0:T(8,128)(2,1)S(1)}, u32[]{:S(2)}, u32[]{:S(2)}) async-start(bf16[4,3,128,256]{3,2,1,0:T(8,128)(2,1)} %get-tuple-element.19), calls=%async_computation | async-start | bytes 1572864 | tf_op jit(solution)/shard_map/all_to_all | solution.py:776
  43.3 0.0 copy-done.1
  43.3 0.0 copy-done.2
  43.3 0.3 place.1.place_ref
  43.7 10.1 %all-to-all-done.grad_ref = bf16[4,3,128,256]{3,2,1,0:T(8,128)(2,1)S(1)} async-done(((bf16[4,3,128,256]{3,2,1,0:T(8,128)(2,1)}), bf16[4,3,128,256]{3,2,1,0:T(8,128)(2,1)S(1)}, u32[]{:S(2)}, u32[]{:S(2)}) %all-to-all-start) | async-done | bytes 786464 | tf_op jit(solution)/shard_map/all_to_all | solution.py:776
  53.8 4.0 %vortex.1 = f32[32,32,128]{2,1,0:T(8,128)} custom-call(bf16[4,3,128,256]{3,2,1,0:T(8,128)(2,1)S(1)} %all-to-all-done.grad_ref, bf16[256,256]{1,0:T(8,128)(2,1)S(1)} %place.1.place_ref), custom_call_target="tpu_custom_call" | custom-call | flops 1000000000 | bytes 2000000 | tf_op jit(solution)/shard_map/vortex/pallas_call | solution.py:788
  57.8 3.7 %all-to-all-start.1 = ((f32[32,32,128]{2,1,0:T(8,128)}), f32[32,32,128]{2,1,0:T(8,128)S(1)}, u32[]{:S(2)}, u32[]{:S(2)}) async-start(f32[32,32,128]{2,1,0:T(8,128)} %vortex.1), calls=%async_computation.1 | async-start | bytes 1048576 | tf_op jit(solution)/shard_map/all_to_all | solution.py:799
  61.5 0.4 slots.1.vel_ref
  62.0 15.8 %all-to-all-done.1 = f32[32,32,128]{2,1,0:T(8,128)S(1)} async-done(((f32[32,32,128]{2,1,0:T(8,128)}), f32[32,32,128]{2,1,0:T(8,128)S(1)}, u32[]{:S(2)}, u32[]{:S(2)}) %all-to-all-start.1) | async-done | bytes 524320 | tf_op jit(solution)/shard_map/all_to_all | solution.py:799
  77.8 0.8 %final.1 = f32[1,256,512]{2,1,0:T(8,128)} custom-call(f32[4,256,128]{2,1,0:T(8,128)S(1)} %bitcast.3, f32[256,512]{1,0:T(8,128)S(1)} %slots.1.vel_ref), custom_call_target="tpu_custom_call" | custom-call | flops 1000000 | bytes 2000000 | tf_op jit(solution)/shard_map/final/pallas_call | solution.py:802
  (2 shorter events, 0.0 us)
Async XLA Ops:
  0.0 3.8 %copy-start.4 = (f32[2,512,128]{2,1,0:T(8,128)S(1)}, f32[2,512,128]{2,1,0:T(8,128)}, u32[]{:S(2)}) copy-start(f32[2,512,128]{2,1,0:T(8,128)} %constant.7.clone.cols_hbm.cols_ref.refs_6_) | copy-start | bytes 1572868
  0.0 5.3 %copy-start.3 = (bf16[6,256,256]{2,1,0:T(8,128)(2,1)S(1)}, bf16[6,256,256]{2,1,0:T(8,128)(2,1)}, u32[]{:S(2)}) copy-start(bf16[6,256,256]{2,1,0:T(8,128)(2,1)} %constant.6.clone.refs_5_) | copy-start | bytes 2359300
  2.5 2.7 %collective-permute-start = (f32[520,256]{1,0:T(8,128)}, f32[520,256]{1,0:T(8,128)S(1)}, u32[]{:S(2)}, u32[]{:S(2)}) collective-permute-start(f32[520,256]{1,0:T(8,128)} %prep.1.own_ref), channel_id=1, source_target_pairs={{0,1},{1,0},{2,3},{3,2},{4,5},{5,4},{6,7},{7,6},{8,9},{9,8},{10,11... | collective-permute-start | bytes 1597448 | tf_op jit(solution)/shard_map/ppermute | solution.py:705
  3.1 2.2 %collective-permute-start.1 = (f32[520,256]{1,0:T(8,128)}, f32[520,256]{1,0:T(8,128)S(1)}, u32[]{:S(2)}, u32[]{:S(2)}) collective-permute-start(f32[520,256]{1,0:T(8,128)} %prep.1.own_ref), channel_id=1, source_target_pairs={{1,2},{2,1},{3,4},{4,3},{5,6},{6,5},{9,10},{10,9},{11,12},{12,11},... | collective-permute-start | bytes 1597448 | tf_op jit(solution)/shard_map/ppermute | solution.py:704
  3.8 1.0 %copy-start = (f32[520,256]{1,0:T(8,128)S(1)}, f32[520,256]{1,0:T(8,128)}, u32[]{:S(2)}) copy-start(f32[520,256]{1,0:T(8,128)} %prep.1.own_ref) | copy-start | bytes 1597444
  5.3 30.9 %copy-start.5 = (f32[8,8,128]{2,1,0:T(8,128)S(1)}, f32[8,8,128]{2,1,0:T(8,128)}, u32[]{:S(2)}) copy-start(f32[8,8,128]{2,1,0:T(8,128)} %constant.8.clone.refs_6_) | copy-start | bytes 98308
  16.0 10.5 %collective-permute-start.2 = (f32[80,128]{1,0:T(8,128)S(1)}, f32[80,128]{1,0:T(8,128)S(1)}, u32[]{:S(2)}, u32[]{:S(2)}) collective-permute-start(f32[80,128]{1,0:T(8,128)S(1)} %get-tuple-element.16), channel_id=1, source_target_pairs={{0,1},{1,0},{2,3},{3,2},{4,5},{5,4},{6,7},{7,6},{8,9},{9,8},{10,11... | collective-permute-start | bytes 122888 | tf_op jit(solution)/shard_map/ppermute | solution.py:756
  25.6 8.8 %collective-permute-start.5 = (f32[80,128]{1,0:T(8,128)S(1)}, f32[80,128]{1,0:T(8,128)S(1)}, u32[]{:S(2)}, u32[]{:S(2)}) collective-permute-start(f32[80,128]{1,0:T(8,128)S(1)} %get-tuple-element.16), channel_id=1, source_target_pairs={{1,2},{2,1},{3,4},{4,3},{5,6},{6,5},{9,10},{10,9},{11,12},{12,11},... | collective-permute-start | bytes 122888 | tf_op jit(solution)/shard_map/ppermute | solution.py:757
  26.5 5.2 %collective-permute-start.3 = (f32[16,128]{1,0:T(8,128)S(1)}, f32[16,128]{1,0:T(8,128)S(1)}, u32[]{:S(2)}, u32[]{:S(2)}) collective-permute-start(f32[16,128]{1,0:T(8,128)S(1)} %slice_add_fusion), channel_id=1, source_target_pairs={{0,2},{1,3},{2,0},{3,1},{4,6},{5,7},{6,4},{7,5},{8,10},{9,11},{10,... | collective-permute-start | bytes 24584 | tf_op jit(solution)/shard_map/ppermute | solution.py:762
  31.7 4.5 %collective-permute-start.4 = (f32[16,128]{1,0:T(8,128)S(1)}, f32[16,128]{1,0:T(8,128)S(1)}, u32[]{:S(2)}, u32[]{:S(2)}) collective-permute-start(f32[16,128]{1,0:T(8,128)S(1)} %add.7.refs_0_), channel_id=1, source_target_pairs={{0,4},{1,5},{2,6},{3,7},{4,0},{5,1},{6,2},{7,3},{8,12},{9,13},{10,... | collective-permute-start | bytes 24584 | tf_op jit(solution)/shard_map/ppermute | solution.py:762
  36.2 7.1 %copy-start.1 = (s32[1,256]{1,0:T(1,128)S(1)}, s32[1,256]{1,0:T(1,128)}, u32[]{:S(2)}) copy-start(s32[1,256]{1,0:T(1,128)} %refs_1_.1) | copy-start | bytes 3076
  36.2 7.1 %copy-start.2 = (s32[1,256]{1,0:T(1,128)S(1)}, s32[1,256]{1,0:T(1,128)}, u32[]{:S(2)}) copy-start(s32[1,256]{1,0:T(1,128)} %order_ref.1) | copy-start | bytes 3076
  39.5 14.2 %all-to-all-start = ((bf16[4,3,128,256]{3,2,1,0:T(8,128)(2,1)}), bf16[4,3,128,256]{3,2,1,0:T(8,128)(2,1)S(1)}, u32[]{:S(2)}, u32[]{:S(2)}) async-start(bf16[4,3,128,256]{3,2,1,0:T(8,128)(2,1)} %get-tuple-element.19), calls=%async_computation | async-start | bytes 1572864 | tf_op jit(solution)/shard_map/all_to_all | solution.py:776
  57.8 19.9 %all-to-all-start.1 = ((f32[32,32,128]{2,1,0:T(8,128)}), f32[32,32,128]{2,1,0:T(8,128)S(1)}, u32[]{:S(2)}, u32[]{:S(2)}) async-start(f32[32,32,128]{2,1,0:T(8,128)} %vortex.1), calls=%async_computation.1 | async-start | bytes 1048576 | tf_op jit(solution)/shard_map/all_to_all | solution.py:799

commit v3 on v2

--- a/solution.py
+++ b/solution.py
@@ -466,11 +466,12 @@
 
 def gradient_kernel(
     diff, sum_a_ref, sum_b_ref, basis_ref, near_ref, fa_ref, fb_ref, dcol_ref,
-    grad_ref, vel_ref, work,
+    *rest,
 ):
+    *grad_refs, vel_ref, work = rest
     elems = basis_ref.shape[2]
-    quarters = grad_ref.shape[0]
-    quarter = grad_ref.shape[2]
+    quarter = grad_refs[0].shape[1]
+    group = lax.axis_index("grp")
     scalars = jnp.sum(sum_a_ref[...] + sum_b_ref[...], axis=1, keepdims=True)
     part = lax.axis_index("dom")
     parts = lax.axis_size("dom")
@@ -518,8 +519,10 @@
                     low_mean = jnp.where(edge, lows[n], low_mean)
                 work[n, last, :] = high_mean
                 work[n, first, :] = low_mean
-        for q in range(quarters):
-            grad_ref[q, direction] = (load_block(work, 0, pl.ds(q * quarter, quarter)) * scale).astype(BF16)
+        for turn, grad_ref in enumerate(grad_refs):
+            start = pl.multiple_of(jnp.bitwise_xor(group, turn) * quarter, quarter)
+            value = load_block(work, 0, pl.ds(start, quarter)) * scale
+            grad_ref[direction] = value.astype(BF16)
 
     @pl.loop(0, NP)
     def _(k):
@@ -621,14 +624,24 @@
     return (d0 + d1 + d2 - largest - smallest) * peak
 
 
-def vortex_kernel(grad_ref, place_ref, out_ref, value):
-    rows_all = grad_ref.shape[2]
+def vortex_kernel(*refs):
+    *grad_refs, place_ref, out_ref, value = refs
+    rows_all = grad_refs[0].shape[1]
+    group = lax.axis_index("grp")
+
+    def component(c, d, rows):
+        turn = jnp.bitwise_xor(group, c)
+        out = grad_refs[-1][d, rows, :].astype(F32)
+        for n in reversed(range(len(grad_refs) - 1)):
+            out = jnp.where(turn == n, grad_refs[n][d, rows, :].astype(F32), out)
+        return out
+
     step = 16
 
     @pl.loop(0, rows_all // step)
     def _(n):
         rows = pl.ds(pl.multiple_of(n * step, step), step)
-        jac = [[grad_ref[c, d, rows, :].astype(F32) for d in range(3)] for c in range(3)]
+        jac = [[component(c, d, rows) for d in range(3)] for c in range(3)]
         value[rows, :] = middle_eigenvalue(jac)
 
     high, mid, low = split3(value[...])
@@ -762,18 +775,21 @@
         pending = (sums, lax.ppermute(sums, "dom", [(i, i ^ reach) for i in range(parts)]))
         reach *= 2
 
-    grads, vel = pl.pallas_call(
+    *grads, vel = pl.pallas_call(
         lambda *refs: gradient_kernel(diff, *refs),
         in_specs=[vmem()] * 7,
-        out_specs=[vmem()] * 2,
-        out_shape=[sds((groups, 3, quarter, elems), BF16), sds((nodes, elems), F32)],
+        out_specs=[vmem()] * (groups + 1),
+        out_shape=[sds((3, quarter, elems), BF16)] * groups + [sds((nodes, elems), F32)],
         scratch_shapes=[pltpu.VMEM((2, nodes, TILE), F32)],
         cost_estimate=cost(10**9, 4 * 10**6),
         compiler_params=GRANT,
         name="gradient",
     )(*pending, basis, near, face_a, face_b, dcol)
 
-    exchanged = lax.all_to_all(grads, "grp", split_axis=0, concat_axis=0, tiled=True)
+    exchanged = [grads[0]] + [
+        lax.ppermute(grads[turn], "grp", [(i, i ^ turn) for i in range(groups)])
+        for turn in range(1, groups)
+    ]
 
     vel_slot = pl.pallas_call(
         slots_kernel,
@@ -787,14 +803,14 @@
 
     packed = pl.pallas_call(
         vortex_kernel,
-        in_specs=[vmem(), vmem()],
+        in_specs=[vmem()] * (groups + 1),
         out_specs=vmem(),
         out_shape=sds((groups * parts, cap, quarter), F32),
         scratch_shapes=[pltpu.VMEM((quarter, elems), F32)],
         cost_estimate=cost(10**9, 2 * 10**6),
         compiler_params=GRANT,
         name="vortex",
-    )(exchanged, place)
+    )(*exchanged, place)
 
     received = lax.all_to_all(
         packed, ("grp", "dom"), split_axis=0, concat_axis=0, tiled=True

time: 78.9 us -> 75.8 us (0.961)
  waiting for transfers between devices: 29.8 us -> 27.6 us
    all_to_all x1 -> x0, waiting for transfers between devices: 10.1 us -> none  [per_device(): lax.all_to_all(grads, 'grp', split_axis=0, concat_axis=0, tiled=True)]
    ppermute x0 -> x3, waiting for transfers between devices: none -> 7.89 us  [per_device(): lax.ppermute(grads[turn], 'grp', [(i, i ^ turn) for i in range(groups)])]
    all_to_all x1 -> x0, starting transfers between devices: 3.78 us -> none  [per_device(): lax.all_to_all(grads, 'grp', split_axis=0, concat_axis=0, tiled=True)]
    ppermute x0 -> x3, starting transfers between devices: none -> 3.55 us  [per_device(): lax.ppermute(grads[turn], 'grp', [(i, i ^ turn) for i in range(groups)])]
    pallas_call x1, Pallas kernels: 3.31 us -> 2.48 us  [per_device(): pl.pallas_call(lambda *refs: gradient_kernel(diff, *refs), in_specs=[vmem...]
  transfers between devices with their start and end apart: 8 -> 10, of which waited for: 5 -> 6; matrix products, arithmetic and copies ran while one was open for 0% -> 0% of each run, Pallas kernels for 2% -> 2%
where the time goes in v3:
time: 75.8 us; the launch traced here: 75.5 us
  waiting for transfers between devices  27.6 us (36%)
  starting transfers between devices  24.8 us (33%)
  Pallas kernels  21.9 us (29%)
  local copies, waits for them, and re-layouts  1.06 us (1%)
    all_to_all x1, waiting for transfers between devices, per_device(): lax.all_to_all(packed, ('grp', 'dom'), split_axis=0, concat_axis=0, tiled...  15.8 us
    pallas_call x1, Pallas kernels, per_device(): pl.pallas_call(lambda *refs: krylov_kernel(diff, bound, *refs), in_specs=...  10.7 us
    ppermute x1, starting transfers between devices, per_device(): face_a = lax.ppermute(message, 'dom', swap_a)  9.6 us
    ppermute x3, waiting for transfers between devices, per_device(): lax.ppermute(grads[turn], 'grp', [(i, i ^ turn) for i in range(groups)])  7.89 us
    ppermute x2, starting transfers between devices, per_device(): lax.ppermute(sums, 'dom', [(i, i ^ reach) for i in range(parts)])  6.02 us
    pallas_call x1, Pallas kernels, per_device(): pl.pallas_call(vortex_kernel, in_specs=[vmem()] * (groups + 1), out_specs...  4.18 us
    ppermute x2, waiting for transfers between devices, per_device(): lax.ppermute(sums, 'dom', [(i, i ^ reach) for i in range(parts)])  3.72 us
    all_to_all x1, starting transfers between devices, per_device(): lax.all_to_all(packed, ('grp', 'dom'), split_axis=0, concat_axis=0, tiled...  3.72 us
  transfers between devices with their start and end apart: 10, of which 6 were waited for; matrix products, arithmetic and copies ran while one was open for 0% of the time, Pallas kernels for 2%

profile of v3, /device:TPU:0, one launch (start us, length us, event | category | flops | bytes accessed | tf_op | source)
XLA Modules:
  0.0 75.5 jit_solution(5825925907509978514)
XLA Ops:
  0.0 0.0 copy-start.4
  0.0 0.0 copy-start.3
  0.0 2.5 %prep.1.own_ref = f32[520,256]{1,0:T(8,128)} custom-call(f32[3,256,512]{2,1,0:T(8,128)} %force_hbm.1, s32[1,256]{1,0:T(1,128)} %order_ref.1, f32[1,256]{1,0:T(1,128)} %bitcast.4, f32[1,256]{1,0:T(1,128)} %bitcast.5, f32[2,512,128]{2,1,0:T(8,128)} %constant.7.clone.cols_hbm.cols_ref.refs_6_), custom_call_target="tpu_custom_call" | custom-call | flops 1000000000 | bytes 2000000 | tf_op jit(solution)/shard_map/prep/pallas_call | solution.py:697
  2.5 0.6 collective-permute-start
  3.1 0.7 collective-permute-start.1
  3.8 0.0 copy-done.4
  3.8 0.0 copy-start
  3.8 1.0 %copy-done = f32[520,256]{1,0:T(8,128)S(1)} copy-done((f32[520,256]{1,0:T(8,128)S(1)}, f32[520,256]{1,0:T(8,128)}, u32[]{:S(2)}) %copy-start) | copy-done | bytes 532504
  4.8 0.4 stage.1
  5.3 0.0 collective-permute-done.refs_3_
  5.3 0.0 collective-permute-done.1.refs_4_
  5.3 0.0 copy-done.3
  5.3 0.0 copy-start.5
  5.3 10.7 %krylov.1 = (f32[4,512,256]{2,1,0:T(8,128)S(1)}, f32[3,64,128]{2,1,0:T(8,128)S(1)}, f32[80,128]{1,0:T(8,128)S(1)}) custom-call(f32[520,256]{1,0:T(8,128)S(1)} %get-tuple-element.16.refs_0_, f32[2,512,128]{2,1,0:T(8,128)S(1)} %get-tuple-element.17.refs_1_, f32[2,512,128]{2,1,0:T(8,128)S(1)} %get-tuple-element.18.refs_2_, ...), custom_call_target="tpu_custom_call" | custom-call | flops 10000000000 | bytes 10000000 | tf_op jit(solution)/shard_map/krylov/pallas_call | solution.py:744
  16.0 0.0 copy-start.1
  16.0 0.0 copy-start.2
  16.0 9.6 %collective-permute-start.2 = (f32[80,128]{1,0:T(8,128)S(1)}, f32[80,128]{1,0:T(8,128)S(1)}, u32[]{:S(2)}, u32[]{:S(2)}) collective-permute-start(f32[80,128]{1,0:T(8,128)S(1)} %get-tuple-element.19), channel_id=1, source_target_pairs={{0,1},{1,0},{2,3},{3,2},{4,5},{5,4},{6,7},{7,6},{8,9},{9,8},{10,11... | collective-permute-start | bytes 122888 | tf_op jit(solution)/shard_map/ppermute | solution.py:769
  25.6 0.7 collective-permute-start.5
  26.3 0.2 collective-permute-done.2.refs_4_
  26.5 3.2 %collective-permute-start.3 = (f32[16,128]{1,0:T(8,128)S(1)}, f32[16,128]{1,0:T(8,128)S(1)}, u32[]{:S(2)}, u32[]{:S(2)}) collective-permute-start(f32[16,128]{1,0:T(8,128)S(1)} %slice_add_fusion), channel_id=1, source_target_pairs={{0,2},{1,3},{2,0},{3,1},{4,6},{5,7},{6,4},{7,5},{8,10},{9,11},{10,... | collective-permute-start | bytes 24584 | tf_op jit(solution)/shard_map/ppermute | solution.py:775
  29.7 2.0 %collective-permute-done.3 = f32[16,128]{1,0:T(8,128)S(1)} collective-permute-done((f32[16,128]{1,0:T(8,128)S(1)}, f32[16,128]{1,0:T(8,128)S(1)}, u32[]{:S(2)}, u32[]{:S(2)}) %collective-permute-start.3) | collective-permute-done | bytes 8224 | tf_op jit(solution)/shard_map/ppermute | solution.py:775
  31.7 2.8 %collective-permute-start.4 = (f32[16,128]{1,0:T(8,128)S(1)}, f32[16,128]{1,0:T(8,128)S(1)}, u32[]{:S(2)}, u32[]{:S(2)}) collective-permute-start(f32[16,128]{1,0:T(8,128)S(1)} %add.7.refs_0_), channel_id=1, source_target_pairs={{0,4},{1,5},{2,6},{3,7},{4,0},{5,1},{6,2},{7,3},{8,12},{9,13},{10,... | collective-permute-start | bytes 24584 | tf_op jit(solution)/shard_map/ppermute | solution.py:775
  34.5 0.0 collective-permute-done.5.refs_5_
  34.5 1.8 %collective-permute-done.4.refs_1_ = f32[16,128]{1,0:T(8,128)S(1)} collective-permute-done((f32[16,128]{1,0:T(8,128)S(1)}, f32[16,128]{1,0:T(8,128)S(1)}, u32[]{:S(2)}, u32[]{:S(2)}) %collective-permute-start.4) | collective-permute-done | bytes 8224 | tf_op jit(solution)/shard_map/ppermute | solution.py:775
  36.2 0.0 copy-done.5
  36.2 2.5 %gradient.1 = (bf16[3,128,256]{2,1,0:T(8,128)(2,1)S(1)}, bf16[3,128,256]{2,1,0:T(8,128)(2,1)S(1)}, bf16[3,128,256]{2,1,0:T(8,128)(2,1)S(1)}, bf16[3,128,256]{2,1,0:T(8,128)(2,1)S(1)}, f32[512,256]{1,0:T(8,128)S(1)}) custom-call(f32[16,128]{1,0:T(8,128)S(1)} %add.7.refs_0_, f32[16,128]{1,0:T(8,128)S(1)} %collective-permute-done.4.refs_1_, ...), custom_call_target="tpu_custom_call" | custom-call | flops 1000000000 | bytes 4000000 | tf_op jit(solution)/shard_map/gradient/pallas_call | solution.py:778
  38.7 1.6 %collective-permute-start.6 = (bf16[3,128,256]{2,1,0:T(8,128)(2,1)S(1)}, bf16[3,128,256]{2,1,0:T(8,128)(2,1)S(1)}, u32[]{:S(2)}, u32[]{:S(2)}) collective-permute-start(bf16[3,128,256]{2,1,0:T(8,128)(2,1)S(1)} %get-tuple-element.23), channel_id=1, source_target_pairs={{0,8},{8,0},{16,24},{24,16},{1,9},{9,1},{17,25},{25,17},{2,10},{10... | collective-permute-start | bytes 589832 | tf_op jit(solution)/shard_map/ppermute | solution.py:790
  40.4 1.5 %collective-permute-start.7 = (bf16[3,128,256]{2,1,0:T(8,128)(2,1)S(1)}, bf16[3,128,256]{2,1,0:T(8,128)(2,1)S(1)}, u32[]{:S(2)}, u32[]{:S(2)}) collective-permute-start(bf16[3,128,256]{2,1,0:T(8,128)(2,1)S(1)} %get-tuple-element.24), channel_id=1, source_target_pairs={{0,16},{8,24},{16,0},{24,8},{1,17},{9,25},{17,1},{25,9},{2,18},{10... | collective-permute-start | bytes 589832 | tf_op jit(solution)/shard_map/ppermute | solution.py:790
  41.9 0.4 collective-permute-start.8
  42.3 0.0 copy-done.1
  42.3 0.0 copy-done.2
  42.3 0.3 place.1.refs_4_
  42.6 3.9 %collective-permute-done.6.refs_1_ = bf16[3,128,256]{2,1,0:T(8,128)(2,1)S(1)} collective-permute-done((bf16[3,128,256]{2,1,0:T(8,128)(2,1)S(1)}, bf16[3,128,256]{2,1,0:T(8,128)(2,1)S(1)}, u32[]{:S(2)}, u32[]{:S(2)}) %collective-permute-start.6) | collective-permute-done | bytes 196640 | tf_op jit(solution)/shard_map/ppermute | solution.py:790
  46.6 4.0 %collective-permute-done.7.refs_2_ = bf16[3,128,256]{2,1,0:T(8,128)(2,1)S(1)} collective-permute-done((bf16[3,128,256]{2,1,0:T(8,128)(2,1)S(1)}, bf16[3,128,256]{2,1,0:T(8,128)(2,1)S(1)}, u32[]{:S(2)}, u32[]{:S(2)}) %collective-permute-start.7) | collective-permute-done | bytes 196640 | tf_op jit(solution)/shard_map/ppermute | solution.py:790
  50.5 0.0 collective-permute-done.8.refs_3_
  50.5 4.2 %vortex.1 = f32[32,32,128]{2,1,0:T(8,128)} custom-call(bf16[3,128,256]{2,1,0:T(8,128)(2,1)S(1)} %get-tuple-element.22.refs_0_, bf16[3,128,256]{2,1,0:T(8,128)(2,1)S(1)} %collective-permute-done.6.refs_1_, bf16[3,128,256]{2,1,0:T(8,128)(2,1)S(1)} %collective-permute-done.7.refs_2_, bf16[3,128,256]{2,1,0:T(8,128)(2,1)S(1)} %collective-permute-done.8.refs_3_, ...), custom_call_target="tpu_custom_call" | custom-call | flops 1000000000 | bytes 2000000 | tf_op jit(solution)/shard_map/vortex/pallas_call | solution.py:804
  54.7 3.7 %all-to-all-start = ((f32[32,32,128]{2,1,0:T(8,128)}), f32[32,32,128]{2,1,0:T(8,128)S(1)}, u32[]{:S(2)}, u32[]{:S(2)}) async-start(f32[32,32,128]{2,1,0:T(8,128)} %vortex.1), calls=%async_computation | async-start | bytes 1048576 | tf_op jit(solution)/shard_map/all_to_all | solution.py:815
  58.4 0.4 slots.1.vel_ref
  58.9 15.8 %all-to-all-done = f32[32,32,128]{2,1,0:T(8,128)S(1)} async-done(((f32[32,32,128]{2,1,0:T(8,128)}), f32[32,32,128]{2,1,0:T(8,128)S(1)}, u32[]{:S(2)}, u32[]{:S(2)}) %all-to-all-start) | async-done | bytes 524320 | tf_op jit(solution)/shard_map/all_to_all | solution.py:815
  74.7 0.8 %final.1 = f32[1,256,512]{2,1,0:T(8,128)} custom-call(f32[4,256,128]{2,1,0:T(8,128)S(1)} %bitcast.3, f32[256,512]{1,0:T(8,128)S(1)} %slots.1.vel_ref), custom_call_target="tpu_custom_call" | custom-call | flops 1000000 | bytes 2000000 | tf_op jit(solution)/shard_map/final/pallas_call | solution.py:818
  (2 shorter events, 0.0 us)
Async XLA Ops:
  0.0 3.8 %copy-start.4 = (f32[2,512,128]{2,1,0:T(8,128)S(1)}, f32[2,512,128]{2,1,0:T(8,128)}, u32[]{:S(2)}) copy-start(f32[2,512,128]{2,1,0:T(8,128)} %constant.7.clone.cols_hbm.cols_ref.refs_6_) | copy-start | bytes 1572868
  0.0 5.3 %copy-start.3 = (bf16[6,256,256]{2,1,0:T(8,128)(2,1)S(1)}, bf16[6,256,256]{2,1,0:T(8,128)(2,1)}, u32[]{:S(2)}) copy-start(bf16[6,256,256]{2,1,0:T(8,128)(2,1)} %constant.6.clone.refs_5_) | copy-start | bytes 2359300
  2.5 2.7 %collective-permute-start = (f32[520,256]{1,0:T(8,128)}, f32[520,256]{1,0:T(8,128)S(1)}, u32[]{:S(2)}, u32[]{:S(2)}) collective-permute-start(f32[520,256]{1,0:T(8,128)} %prep.1.own_ref), channel_id=1, source_target_pairs={{0,1},{1,0},{2,3},{3,2},{4,5},{5,4},{6,7},{7,6},{8,9},{9,8},{10,11... | collective-permute-start | bytes 1597448 | tf_op jit(solution)/shard_map/ppermute | solution.py:718
  3.1 2.2 %collective-permute-start.1 = (f32[520,256]{1,0:T(8,128)}, f32[520,256]{1,0:T(8,128)S(1)}, u32[]{:S(2)}, u32[]{:S(2)}) collective-permute-start(f32[520,256]{1,0:T(8,128)} %prep.1.own_ref), channel_id=1, source_target_pairs={{1,2},{2,1},{3,4},{4,3},{5,6},{6,5},{9,10},{10,9},{11,12},{12,11},... | collective-permute-start | bytes 1597448 | tf_op jit(solution)/shard_map/ppermute | solution.py:717
  3.8 1.0 %copy-start = (f32[520,256]{1,0:T(8,128)S(1)}, f32[520,256]{1,0:T(8,128)}, u32[]{:S(2)}) copy-start(f32[520,256]{1,0:T(8,128)} %prep.1.own_ref) | copy-start | bytes 1597444
  5.3 31.0 %copy-start.5 = (f32[8,8,128]{2,1,0:T(8,128)S(1)}, f32[8,8,128]{2,1,0:T(8,128)}, u32[]{:S(2)}) copy-start(f32[8,8,128]{2,1,0:T(8,128)} %constant.8.clone.refs_6_) | copy-start | bytes 98308
  16.0 26.3 %copy-start.1 = (s32[1,256]{1,0:T(1,128)S(1)}, s32[1,256]{1,0:T(1,128)}, u32[]{:S(2)}) copy-start(s32[1,256]{1,0:T(1,128)} %refs_1_.1) | copy-start | bytes 3076
  16.0 26.3 %copy-start.2 = (s32[1,256]{1,0:T(1,128)S(1)}, s32[1,256]{1,0:T(1,128)}, u32[]{:S(2)}) copy-start(s32[1,256]{1,0:T(1,128)} %order_ref.1) | copy-start | bytes 3076
  16.0 10.5 %collective-permute-start.2 = (f32[80,128]{1,0:T(8,128)S(1)}, f32[80,128]{1,0:T(8,128)S(1)}, u32[]{:S(2)}, u32[]{:S(2)}) collective-permute-start(f32[80,128]{1,0:T(8,128)S(1)} %get-tuple-element.19), channel_id=1, source_target_pairs={{0,1},{1,0},{2,3},{3,2},{4,5},{5,4},{6,7},{7,6},{8,9},{9,8},{10,11... | collective-permute-start | bytes 122888 | tf_op jit(solution)/shard_map/ppermute | solution.py:769
  25.6 8.9 %collective-permute-start.5 = (f32[80,128]{1,0:T(8,128)S(1)}, f32[80,128]{1,0:T(8,128)S(1)}, u32[]{:S(2)}, u32[]{:S(2)}) collective-permute-start(f32[80,128]{1,0:T(8,128)S(1)} %get-tuple-element.19), channel_id=1, source_target_pairs={{1,2},{2,1},{3,4},{4,3},{5,6},{6,5},{9,10},{10,9},{11,12},{12,11},... | collective-permute-start | bytes 122888 | tf_op jit(solution)/shard_map/ppermute | solution.py:770
  26.5 5.2 %collective-permute-start.3 = (f32[16,128]{1,0:T(8,128)S(1)}, f32[16,128]{1,0:T(8,128)S(1)}, u32[]{:S(2)}, u32[]{:S(2)}) collective-permute-start(f32[16,128]{1,0:T(8,128)S(1)} %slice_add_fusion), channel_id=1, source_target_pairs={{0,2},{1,3},{2,0},{3,1},{4,6},{5,7},{6,4},{7,5},{8,10},{9,11},{10,... | collective-permute-start | bytes 24584 | tf_op jit(solution)/shard_map/ppermute | solution.py:775
  31.7 4.5 %collective-permute-start.4 = (f32[16,128]{1,0:T(8,128)S(1)}, f32[16,128]{1,0:T(8,128)S(1)}, u32[]{:S(2)}, u32[]{:S(2)}) collective-permute-start(f32[16,128]{1,0:T(8,128)S(1)} %add.7.refs_0_), channel_id=1, source_target_pairs={{0,4},{1,5},{2,6},{3,7},{4,0},{5,1},{6,2},{7,3},{8,12},{9,13},{10,... | collective-permute-start | bytes 24584 | tf_op jit(solution)/shard_map/ppermute | solution.py:775
  38.7 7.8 %collective-permute-start.6 = (bf16[3,128,256]{2,1,0:T(8,128)(2,1)S(1)}, bf16[3,128,256]{2,1,0:T(8,128)(2,1)S(1)}, u32[]{:S(2)}, u32[]{:S(2)}) collective-permute-start(bf16[3,128,256]{2,1,0:T(8,128)(2,1)S(1)} %get-tuple-element.23), channel_id=1, source_target_pairs={{0,8},{8,0},{16,24},{24,16},{1,9},{9,1},{17,25},{25,17},{2,10},{10... | collective-permute-start | bytes 589832 | tf_op jit(solution)/shard_map/ppermute | solution.py:790
  40.4 10.2 %collective-permute-start.7 = (bf16[3,128,256]{2,1,0:T(8,128)(2,1)S(1)}, bf16[3,128,256]{2,1,0:T(8,128)(2,1)S(1)}, u32[]{:S(2)}, u32[]{:S(2)}) collective-permute-start(bf16[3,128,256]{2,1,0:T(8,128)(2,1)S(1)} %get-tuple-element.24), channel_id=1, source_target_pairs={{0,16},{8,24},{16,0},{24,8},{1,17},{9,25},{17,1},{25,9},{2,18},{10... | collective-permute-start | bytes 589832 | tf_op jit(solution)/shard_map/ppermute | solution.py:790
  41.9 8.6 %collective-permute-start.8 = (bf16[3,128,256]{2,1,0:T(8,128)(2,1)S(1)}, bf16[3,128,256]{2,1,0:T(8,128)(2,1)S(1)}, u32[]{:S(2)}, u32[]{:S(2)}) collective-permute-start(bf16[3,128,256]{2,1,0:T(8,128)(2,1)S(1)} %get-tuple-element.25), channel_id=1, source_target_pairs={{0,24},{8,16},{16,8},{24,0},{1,25},{9,17},{17,9},{25,1},{2,26},{10... | collective-permute-start | bytes 589832 | tf_op jit(solution)/shard_map/ppermute | solution.py:790
  54.7 20.0 %all-to-all-start = ((f32[32,32,128]{2,1,0:T(8,128)}), f32[32,32,128]{2,1,0:T(8,128)S(1)}, u32[]{:S(2)}, u32[]{:S(2)}) async-start(f32[32,32,128]{2,1,0:T(8,128)} %vortex.1), calls=%async_computation | async-start | bytes 1048576 | tf_op jit(solution)/shard_map/all_to_all | solution.py:815

commit v4 on v3

--- a/solution.py
+++ b/solution.py
@@ -647,22 +647,20 @@
     high, mid, low = split3(value[...])
     place = place_ref[...]
     moved = dot_nt(place, high) + dot_nt(place, mid) + dot_nt(place, low)
-    owners, cap = out_ref.shape[0], out_ref.shape[1]
-    used = place.shape[0] // cap
-    out_ref[: owners - used] = jnp.zeros((owners - used,) + out_ref.shape[1:], F32)
-    out_ref[owners - used :] = moved.reshape((used,) + out_ref.shape[1:])
-
-
-def final_kernel(vortex_ref, vel_ref, out_ref):
-    quarters = vortex_ref.shape[0]
-    quarter = vortex_ref.shape[2]
+    out_ref[...] = moved.reshape(out_ref.shape)
+
+
+def final_kernel(*refs):
+    *vortex_refs, vel_ref, out_ref = refs
+    quarters = len(vortex_refs)
+    quarter = vortex_refs[0].shape[1]
 
     last = lax.axis_index("grp") == lax.axis_size("grp") - 1
 
     @pl.when(last)
     def _():
         for q in range(quarters):
-            out_ref[0, :, q * quarter : (q + 1) * quarter] = vortex_ref[q]
+            out_ref[0, :, q * quarter : (q + 1) * quarter] = vortex_refs[(quarters - 1) ^ q][...]
 
     @pl.when(jnp.logical_not(last))
     def _():
@@ -805,25 +803,28 @@
         vortex_kernel,
         in_specs=[vmem()] * (groups + 1),
         out_specs=vmem(),
-        out_shape=sds((groups * parts, cap, quarter), F32),
+        out_shape=sds((parts, cap, quarter), F32),
         scratch_shapes=[pltpu.VMEM((quarter, elems), F32)],
         cost_estimate=cost(10**9, 2 * 10**6),
         compiler_params=GRANT,
         name="vortex",
     )(*exchanged, place)
 
-    received = lax.all_to_all(
-        packed, ("grp", "dom"), split_axis=0, concat_axis=0, tiled=True
-    )
+    received = lax.all_to_all(packed, "dom", split_axis=0, concat_axis=0, tiled=True)
+    received = received.reshape(elems, quarter)
+    gathered = [received] + [
+        lax.ppermute(received, "grp", [(i, i ^ turn) for i in range(groups)])
+        for turn in range(1, groups)
+    ]
     return pl.pallas_call(
         final_kernel,
-        in_specs=[vmem(), vmem()],
+        in_specs=[vmem()] * (groups + 1),
         out_specs=vmem(),
         out_shape=sds((1, elems, nodes), F32),
         cost_estimate=cost(10**6, 2 * 10**6),
         compiler_params=GRANT,
         name="final",
-    )(received.reshape(groups, elems, quarter), vel_slot)
+    )(*gathered, vel_slot)
 
 
 def solution(mesh):

time: 75.8 us -> 74.4 us (0.982)
  waiting for transfers between devices: 27.6 us -> 16.8 us
  blocking collectives: 0 us -> 10.5 us
  Pallas kernels: 21.9 us -> 21.1 us
    all_to_all x1 -> x0, waiting for transfers between devices: 15.8 us -> none  [per_device(): lax.all_to_all(packed, ('grp', 'dom'), split_axis=0, concat_axis=0, tiled...]
    all_to_all x0 -> x1, blocking collectives: none -> 10.5 us  [per_device(): lax.all_to_all(packed, 'dom', split_axis=0, concat_axis=0, tiled=True)]
    ppermute x0 -> x3, waiting for transfers between devices: none -> 5 us  [per_device(): lax.ppermute(received, 'grp', [(i, i ^ turn) for i in range(groups)])]
    all_to_all x1 -> x0, starting transfers between devices: 3.72 us -> none  [per_device(): lax.all_to_all(packed, ('grp', 'dom'), split_axis=0, concat_axis=0, tiled...]
    ppermute x0 -> x3, starting transfers between devices: none -> 3.49 us  [per_device(): lax.ppermute(received, 'grp', [(i, i ^ turn) for i in range(groups)])]
    pallas_call x1, Pallas kernels: 4.18 us -> 3.38 us  [per_device(): pl.pallas_call(vortex_kernel, in_specs=[vmem()] * (groups + 1), out_specs...]
  transfers between devices with their start and end apart: 10 -> 12, of which waited for: 6 -> 8; matrix products, arithmetic and copies ran while one was open for 0% -> 0% of each run, Pallas kernels for 2% -> 2%
where the time goes in v4:
time: 74.4 us; the launch traced here: 74.2 us
  starting transfers between devices  24.6 us (33%)
  Pallas kernels  21.1 us (28%)
  waiting for transfers between devices  16.8 us (23%)
  blocking collectives  10.5 us (14%)
  local copies, waits for them, and re-layouts  1.06 us (1%)
    pallas_call x1, Pallas kernels, per_device(): pl.pallas_call(lambda *refs: krylov_kernel(diff, bound, *refs), in_specs=...  10.7 us
    all_to_all x1, blocking collectives, per_device(): lax.all_to_all(packed, 'dom', split_axis=0, concat_axis=0, tiled=True)  10.5 us
    ppermute x1, starting transfers between devices, per_device(): face_a = lax.ppermute(message, 'dom', swap_a)  9.61 us
    ppermute x3, waiting for transfers between devices, per_device(): lax.ppermute(grads[turn], 'grp', [(i, i ^ turn) for i in range(groups)])  7.89 us
    ppermute x2, starting transfers between devices, per_device(): lax.ppermute(sums, 'dom', [(i, i ^ reach) for i in range(parts)])  6.01 us
    ppermute x3, waiting for transfers between devices, per_device(): lax.ppermute(received, 'grp', [(i, i ^ turn) for i in range(groups)])  5 us
    ppermute x2, waiting for transfers between devices, per_device(): lax.ppermute(sums, 'dom', [(i, i ^ reach) for i in range(parts)])  3.72 us
    ppermute x3, starting transfers between devices, per_device(): lax.ppermute(grads[turn], 'grp', [(i, i ^ turn) for i in range(groups)])  3.55 us
  transfers between devices with their start and end apart: 12, of which 8 were waited for; matrix products, arithmetic and copies ran while one was open for 0% of the time, Pallas kernels for 2%

profile of v4, /device:TPU:0, one launch (start us, length us, event | category | flops | bytes accessed | tf_op | source)
XLA Modules:
  0.0 74.2 jit_solution(9745627894471926600)
XLA Ops:
  0.0 0.0 copy-start.4
  0.0 0.0 copy-start.3
  0.0 2.5 %prep.1.own_ref = f32[520,256]{1,0:T(8,128)} custom-call(f32[3,256,512]{2,1,0:T(8,128)} %force_hbm.1, s32[1,256]{1,0:T(1,128)} %order_ref.1, f32[1,256]{1,0:T(1,128)} %bitcast.7, f32[1,256]{1,0:T(1,128)} %bitcast.8, f32[2,512,128]{2,1,0:T(8,128)} %constant.7.clone.cols_hbm.cols_ref.refs_6_), custom_call_target="tpu_custom_call" | custom-call | flops 1000000000 | bytes 2000000 | tf_op jit(solution)/shard_map/prep/pallas_call | solution.py:695
  2.5 0.6 collective-permute-start
  3.1 0.7 collective-permute-start.1
  3.8 0.0 copy-done.4
  3.8 0.0 copy-start
  3.8 1.0 %copy-done = f32[520,256]{1,0:T(8,128)S(1)} copy-done((f32[520,256]{1,0:T(8,128)S(1)}, f32[520,256]{1,0:T(8,128)}, u32[]{:S(2)}) %copy-start) | copy-done | bytes 532504
  4.8 0.4 stage.1
  5.3 0.0 collective-permute-done.refs_3_
  5.3 0.0 collective-permute-done.1.refs_4_
  5.3 0.0 copy-done.3
  5.3 0.0 copy-start.5
  5.3 10.7 %krylov.1 = (f32[4,512,256]{2,1,0:T(8,128)S(1)}, f32[3,64,128]{2,1,0:T(8,128)S(1)}, f32[80,128]{1,0:T(8,128)S(1)}) custom-call(f32[520,256]{1,0:T(8,128)S(1)} %get-tuple-element.16.refs_0_, f32[2,512,128]{2,1,0:T(8,128)S(1)} %get-tuple-element.17.refs_1_, f32[2,512,128]{2,1,0:T(8,128)S(1)} %get-tuple-element.18.refs_2_, ...), custom_call_target="tpu_custom_call" | custom-call | flops 10000000000 | bytes 10000000 | tf_op jit(solution)/shard_map/krylov/pallas_call | solution.py:742
  16.0 0.0 copy-start.1
  16.0 0.0 copy-start.2
  16.0 9.6 %collective-permute-start.2 = (f32[80,128]{1,0:T(8,128)S(1)}, f32[80,128]{1,0:T(8,128)S(1)}, u32[]{:S(2)}, u32[]{:S(2)}) collective-permute-start(f32[80,128]{1,0:T(8,128)S(1)} %get-tuple-element.19), channel_id=1, source_target_pairs={{0,1},{1,0},{2,3},{3,2},{4,5},{5,4},{6,7},{7,6},{8,9},{9,8},{10,11... | collective-permute-start | bytes 122888 | tf_op jit(solution)/shard_map/ppermute | solution.py:767
  25.6 0.7 collective-permute-start.5
  26.3 0.2 collective-permute-done.2.refs_4_
  26.5 3.2 %collective-permute-start.3 = (f32[16,128]{1,0:T(8,128)S(1)}, f32[16,128]{1,0:T(8,128)S(1)}, u32[]{:S(2)}, u32[]{:S(2)}) collective-permute-start(f32[16,128]{1,0:T(8,128)S(1)} %slice_add_fusion), channel_id=1, source_target_pairs={{0,2},{1,3},{2,0},{3,1},{4,6},{5,7},{6,4},{7,5},{8,10},{9,11},{10,... | collective-permute-start | bytes 24584 | tf_op jit(solution)/shard_map/ppermute | solution.py:773
  29.7 2.0 %collective-permute-done.3 = f32[16,128]{1,0:T(8,128)S(1)} collective-permute-done((f32[16,128]{1,0:T(8,128)S(1)}, f32[16,128]{1,0:T(8,128)S(1)}, u32[]{:S(2)}, u32[]{:S(2)}) %collective-permute-start.3) | collective-permute-done | bytes 8224 | tf_op jit(solution)/shard_map/ppermute | solution.py:773
  31.7 2.8 %collective-permute-start.4 = (f32[16,128]{1,0:T(8,128)S(1)}, f32[16,128]{1,0:T(8,128)S(1)}, u32[]{:S(2)}, u32[]{:S(2)}) collective-permute-start(f32[16,128]{1,0:T(8,128)S(1)} %add.7.refs_0_), channel_id=1, source_target_pairs={{0,4},{1,5},{2,6},{3,7},{4,0},{5,1},{6,2},{7,3},{8,12},{9,13},{10,... | collective-permute-start | bytes 24584 | tf_op jit(solution)/shard_map/ppermute | solution.py:773
  34.5 0.0 collective-permute-done.5.refs_5_
  34.5 1.8 %collective-permute-done.4.refs_1_ = f32[16,128]{1,0:T(8,128)S(1)} collective-permute-done((f32[16,128]{1,0:T(8,128)S(1)}, f32[16,128]{1,0:T(8,128)S(1)}, u32[]{:S(2)}, u32[]{:S(2)}) %collective-permute-start.4) | collective-permute-done | bytes 8224 | tf_op jit(solution)/shard_map/ppermute | solution.py:773
  36.2 0.0 copy-done.5
  36.2 2.5 %gradient.1 = (bf16[3,128,256]{2,1,0:T(8,128)(2,1)S(1)}, bf16[3,128,256]{2,1,0:T(8,128)(2,1)S(1)}, bf16[3,128,256]{2,1,0:T(8,128)(2,1)S(1)}, bf16[3,128,256]{2,1,0:T(8,128)(2,1)S(1)}, f32[512,256]{1,0:T(8,128)S(1)}) custom-call(f32[16,128]{1,0:T(8,128)S(1)} %add.7.refs_0_, f32[16,128]{1,0:T(8,128)S(1)} %collective-permute-done.4.refs_1_, ...), custom_call_target="tpu_custom_call" | custom-call | flops 1000000000 | bytes 4000000 | tf_op jit(solution)/shard_map/gradient/pallas_call | solution.py:776
  38.7 1.6 %collective-permute-start.6 = (bf16[3,128,256]{2,1,0:T(8,128)(2,1)S(1)}, bf16[3,128,256]{2,1,0:T(8,128)(2,1)S(1)}, u32[]{:S(2)}, u32[]{:S(2)}) collective-permute-start(bf16[3,128,256]{2,1,0:T(8,128)(2,1)S(1)} %get-tuple-element.23), channel_id=1, source_target_pairs={{0,8},{8,0},{16,24},{24,16},{1,9},{9,1},{17,25},{25,17},{2,10},{10... | collective-permute-start | bytes 589832 | tf_op jit(solution)/shard_map/ppermute | solution.py:788
  40.3 1.5 %collective-permute-start.7 = (bf16[3,128,256]{2,1,0:T(8,128)(2,1)S(1)}, bf16[3,128,256]{2,1,0:T(8,128)(2,1)S(1)}, u32[]{:S(2)}, u32[]{:S(2)}) collective-permute-start(bf16[3,128,256]{2,1,0:T(8,128)(2,1)S(1)} %get-tuple-element.24), channel_id=1, source_target_pairs={{0,16},{8,24},{16,0},{24,8},{1,17},{9,25},{17,1},{25,9},{2,18},{10... | collective-permute-start | bytes 589832 | tf_op jit(solution)/shard_map/ppermute | solution.py:788
  41.9 0.4 collective-permute-start.8
  42.3 0.0 copy-done.1
  42.3 0.0 copy-done.2
  42.3 0.3 place.1.refs_4_
  42.6 3.9 %collective-permute-done.6.refs_1_ = bf16[3,128,256]{2,1,0:T(8,128)(2,1)S(1)} collective-permute-done((bf16[3,128,256]{2,1,0:T(8,128)(2,1)S(1)}, bf16[3,128,256]{2,1,0:T(8,128)(2,1)S(1)}, u32[]{:S(2)}, u32[]{:S(2)}) %collective-permute-start.6) | collective-permute-done | bytes 196640 | tf_op jit(solution)/shard_map/ppermute | solution.py:788
  46.6 4.0 %collective-permute-done.7.refs_2_ = bf16[3,128,256]{2,1,0:T(8,128)(2,1)S(1)} collective-permute-done((bf16[3,128,256]{2,1,0:T(8,128)(2,1)S(1)}, bf16[3,128,256]{2,1,0:T(8,128)(2,1)S(1)}, u32[]{:S(2)}, u32[]{:S(2)}) %collective-permute-start.7) | collective-permute-done | bytes 196640 | tf_op jit(solution)/shard_map/ppermute | solution.py:788
  50.5 0.0 collective-permute-done.8.refs_3_
  50.5 3.4 %vortex.1 = f32[8,32,128]{2,1,0:T(8,128)S(1)} custom-call(bf16[3,128,256]{2,1,0:T(8,128)(2,1)S(1)} %get-tuple-element.22.refs_0_, bf16[3,128,256]{2,1,0:T(8,128)(2,1)S(1)} %collective-permute-done.6.refs_1_, bf16[3,128,256]{2,1,0:T(8,128)(2,1)S(1)} %collective-permute-done.7.refs_2_, bf16[3,128,256]{2,1,0:T(8,128)(2,1)S(1)} %collective-permute-done.8.refs_3_, ...), custom_call_target="tpu_custom_call" | custom-call | flops 1000000000 | bytes 2000000 | tf_op jit(solution)/shard_map/vortex/pallas_call | solution.py:802
  53.9 10.5 %all_to_all.5 = f32[8,32,128]{2,1,0:T(8,128)S(1)} all-to-all(f32[8,32,128]{2,1,0:T(8,128)S(1)} %vortex.1), channel_id=1, replica_groups=mesh['grp'=4,'dom'=8] {'dom'}, dimensions={0} | all-to-all | bytes 262144 | tf_op jit(solution)/shard_map/all_to_all | solution.py:813
  64.4 1.2 %collective-permute-start.10 = (f32[256,128]{1,0:T(8,128)S(1)}, f32[256,128]{1,0:T(8,128)S(1)}, u32[]{:S(2)}, u32[]{:S(2)}) collective-permute-start(f32[256,128]{1,0:T(8,128)S(1)} %bitcast.3), channel_id=1, source_target_pairs={{0,16},{8,24},{16,0},{24,8},{1,17},{9,25},{17,1},{25,9},{2,18},{10... | collective-permute-start | bytes 393224 | tf_op jit(solution)/shard_map/ppermute | solution.py:816
  65.6 1.2 %collective-permute-start.11 = (f32[256,128]{1,0:T(8,128)S(1)}, f32[256,128]{1,0:T(8,128)S(1)}, u32[]{:S(2)}, u32[]{:S(2)}) collective-permute-start(f32[256,128]{1,0:T(8,128)S(1)} %bitcast.4), channel_id=1, source_target_pairs={{0,24},{8,16},{16,8},{24,0},{1,25},{9,17},{17,9},{25,1},{2,26},{10... | collective-permute-start | bytes 393224 | tf_op jit(solution)/shard_map/ppermute | solution.py:816
  66.8 1.1 %collective-permute-start.9 = (f32[256,128]{1,0:T(8,128)S(1)}, f32[256,128]{1,0:T(8,128)S(1)}, u32[]{:S(2)}, u32[]{:S(2)}) collective-permute-start(f32[256,128]{1,0:T(8,128)S(1)} %bitcast.5), channel_id=1, source_target_pairs={{0,8},{8,0},{16,24},{24,16},{1,9},{9,1},{17,25},{25,17},{2,10},{10... | collective-permute-start | bytes 393224 | tf_op jit(solution)/shard_map/ppermute | solution.py:816
  67.9 0.4 slots.1.refs_4_
  68.4 3.1 %collective-permute-done.10.refs_2_ = f32[256,128]{1,0:T(8,128)S(1)} collective-permute-done((f32[256,128]{1,0:T(8,128)S(1)}, f32[256,128]{1,0:T(8,128)S(1)}, u32[]{:S(2)}, u32[]{:S(2)}) %collective-permute-start.10) | collective-permute-done | bytes 131104 | tf_op jit(solution)/shard_map/ppermute | solution.py:816
  71.5 1.2 %collective-permute-done.11.refs_3_ = f32[256,128]{1,0:T(8,128)S(1)} collective-permute-done((f32[256,128]{1,0:T(8,128)S(1)}, f32[256,128]{1,0:T(8,128)S(1)}, u32[]{:S(2)}, u32[]{:S(2)}) %collective-permute-start.11) | collective-permute-done | bytes 131104 | tf_op jit(solution)/shard_map/ppermute | solution.py:816
  72.7 0.7 collective-permute-done.9.refs_1_
  73.3 0.8 %final.1 = f32[1,256,512]{2,1,0:T(8,128)} custom-call(f32[256,128]{1,0:T(8,128)S(1)} %bitcast.6, f32[256,128]{1,0:T(8,128)S(1)} %collective-permute-done.9.refs_1_, f32[256,128]{1,0:T(8,128)S(1)} %collective-permute-done.10.refs_2_, f32[256,128]{1,0:T(8,128)S(1)} %collective-permute-done.11.refs_3_, f32[256,512]{1,0:T(8,128)S(1)} %slots.1.refs_4_), custom_call_target="tpu_custom_call" | custom-call | flops 1000000 | bytes 2000000 | tf_op jit(solution)/shard_map/final/pallas_call | solution.py:819
  (2 shorter events, 0.0 us)
Async XLA Ops:
  0.0 3.8 %copy-start.4 = (f32[2,512,128]{2,1,0:T(8,128)S(1)}, f32[2,512,128]{2,1,0:T(8,128)}, u32[]{:S(2)}) copy-start(f32[2,512,128]{2,1,0:T(8,128)} %constant.7.clone.cols_hbm.cols_ref.refs_6_) | copy-start | bytes 1572868
  0.0 5.3 %copy-start.3 = (bf16[6,256,256]{2,1,0:T(8,128)(2,1)S(1)}, bf16[6,256,256]{2,1,0:T(8,128)(2,1)}, u32[]{:S(2)}) copy-start(bf16[6,256,256]{2,1,0:T(8,128)(2,1)} %constant.6.clone.refs_5_) | copy-start | bytes 2359300
  2.5 2.7 %collective-permute-start = (f32[520,256]{1,0:T(8,128)}, f32[520,256]{1,0:T(8,128)S(1)}, u32[]{:S(2)}, u32[]{:S(2)}) collective-permute-start(f32[520,256]{1,0:T(8,128)} %prep.1.own_ref), channel_id=1, source_target_pairs={{0,1},{1,0},{2,3},{3,2},{4,5},{5,4},{6,7},{7,6},{8,9},{9,8},{10,11... | collective-permute-start | bytes 1597448 | tf_op jit(solution)/shard_map/ppermute | solution.py:716
  3.1 2.2 %collective-permute-start.1 = (f32[520,256]{1,0:T(8,128)}, f32[520,256]{1,0:T(8,128)S(1)}, u32[]{:S(2)}, u32[]{:S(2)}) collective-permute-start(f32[520,256]{1,0:T(8,128)} %prep.1.own_ref), channel_id=1, source_target_pairs={{1,2},{2,1},{3,4},{4,3},{5,6},{6,5},{9,10},{10,9},{11,12},{12,11},... | collective-permute-start | bytes 1597448 | tf_op jit(solution)/shard_map/ppermute | solution.py:715
  3.8 1.0 %copy-start = (f32[520,256]{1,0:T(8,128)S(1)}, f32[520,256]{1,0:T(8,128)}, u32[]{:S(2)}) copy-start(f32[520,256]{1,0:T(8,128)} %prep.1.own_ref) | copy-start | bytes 1597444
  5.3 31.0 %copy-start.5 = (f32[8,8,128]{2,1,0:T(8,128)S(1)}, f32[8,8,128]{2,1,0:T(8,128)}, u32[]{:S(2)}) copy-start(f32[8,8,128]{2,1,0:T(8,128)} %constant.8.clone.refs_6_) | copy-start | bytes 98308
  16.0 26.3 %copy-start.1 = (s32[1,256]{1,0:T(1,128)S(1)}, s32[1,256]{1,0:T(1,128)}, u32[]{:S(2)}) copy-start(s32[1,256]{1,0:T(1,128)} %refs_1_.1) | copy-start | bytes 3076
  16.0 26.3 %copy-start.2 = (s32[1,256]{1,0:T(1,128)S(1)}, s32[1,256]{1,0:T(1,128)}, u32[]{:S(2)}) copy-start(s32[1,256]{1,0:T(1,128)} %order_ref.1) | copy-start | bytes 3076
  16.0 10.5 %collective-permute-start.2 = (f32[80,128]{1,0:T(8,128)S(1)}, f32[80,128]{1,0:T(8,128)S(1)}, u32[]{:S(2)}, u32[]{:S(2)}) collective-permute-start(f32[80,128]{1,0:T(8,128)S(1)} %get-tuple-element.19), channel_id=1, source_target_pairs={{0,1},{1,0},{2,3},{3,2},{4,5},{5,4},{6,7},{7,6},{8,9},{9,8},{10,11... | collective-permute-start | bytes 122888 | tf_op jit(solution)/shard_map/ppermute | solution.py:767
  25.6 8.8 %collective-permute-start.5 = (f32[80,128]{1,0:T(8,128)S(1)}, f32[80,128]{1,0:T(8,128)S(1)}, u32[]{:S(2)}, u32[]{:S(2)}) collective-permute-start(f32[80,128]{1,0:T(8,128)S(1)} %get-tuple-element.19), channel_id=1, source_target_pairs={{1,2},{2,1},{3,4},{4,3},{5,6},{6,5},{9,10},{10,9},{11,12},{12,11},... | collective-permute-start | bytes 122888 | tf_op jit(solution)/shard_map/ppermute | solution.py:768
  26.5 5.2 %collective-permute-start.3 = (f32[16,128]{1,0:T(8,128)S(1)}, f32[16,128]{1,0:T(8,128)S(1)}, u32[]{:S(2)}, u32[]{:S(2)}) collective-permute-start(f32[16,128]{1,0:T(8,128)S(1)} %slice_add_fusion), channel_id=1, source_target_pairs={{0,2},{1,3},{2,0},{3,1},{4,6},{5,7},{6,4},{7,5},{8,10},{9,11},{10,... | collective-permute-start | bytes 24584 | tf_op jit(solution)/shard_map/ppermute | solution.py:773
  31.7 4.5 %collective-permute-start.4 = (f32[16,128]{1,0:T(8,128)S(1)}, f32[16,128]{1,0:T(8,128)S(1)}, u32[]{:S(2)}, u32[]{:S(2)}) collective-permute-start(f32[16,128]{1,0:T(8,128)S(1)} %add.7.refs_0_), channel_id=1, source_target_pairs={{0,4},{1,5},{2,6},{3,7},{4,0},{5,1},{6,2},{7,3},{8,12},{9,13},{10,... | collective-permute-start | bytes 24584 | tf_op jit(solution)/shard_map/ppermute | solution.py:773
  38.7 7.8 %collective-permute-start.6 = (bf16[3,128,256]{2,1,0:T(8,128)(2,1)S(1)}, bf16[3,128,256]{2,1,0:T(8,128)(2,1)S(1)}, u32[]{:S(2)}, u32[]{:S(2)}) collective-permute-start(bf16[3,128,256]{2,1,0:T(8,128)(2,1)S(1)} %get-tuple-element.23), channel_id=1, source_target_pairs={{0,8},{8,0},{16,24},{24,16},{1,9},{9,1},{17,25},{25,17},{2,10},{10... | collective-permute-start | bytes 589832 | tf_op jit(solution)/shard_map/ppermute | solution.py:788
  40.3 10.2 %collective-permute-start.7 = (bf16[3,128,256]{2,1,0:T(8,128)(2,1)S(1)}, bf16[3,128,256]{2,1,0:T(8,128)(2,1)S(1)}, u32[]{:S(2)}, u32[]{:S(2)}) collective-permute-start(bf16[3,128,256]{2,1,0:T(8,128)(2,1)S(1)} %get-tuple-element.24), channel_id=1, source_target_pairs={{0,16},{8,24},{16,0},{24,8},{1,17},{9,25},{17,1},{25,9},{2,18},{10... | collective-permute-start | bytes 589832 | tf_op jit(solution)/shard_map/ppermute | solution.py:788
  41.9 8.6 %collective-permute-start.8 = (bf16[3,128,256]{2,1,0:T(8,128)(2,1)S(1)}, bf16[3,128,256]{2,1,0:T(8,128)(2,1)S(1)}, u32[]{:S(2)}, u32[]{:S(2)}) collective-permute-start(bf16[3,128,256]{2,1,0:T(8,128)(2,1)S(1)} %get-tuple-element.25), channel_id=1, source_target_pairs={{0,24},{8,16},{16,8},{24,0},{1,25},{9,17},{17,9},{25,1},{2,26},{10... | collective-permute-start | bytes 589832 | tf_op jit(solution)/shard_map/ppermute | solution.py:788
  64.4 7.1 %collective-permute-start.10 = (f32[256,128]{1,0:T(8,128)S(1)}, f32[256,128]{1,0:T(8,128)S(1)}, u32[]{:S(2)}, u32[]{:S(2)}) collective-permute-start(f32[256,128]{1,0:T(8,128)S(1)} %bitcast.3), channel_id=1, source_target_pairs={{0,16},{8,24},{16,0},{24,8},{1,17},{9,25},{17,1},{25,9},{2,18},{10... | collective-permute-start | bytes 393224 | tf_op jit(solution)/shard_map/ppermute | solution.py:816
  65.6 7.0 %collective-permute-start.11 = (f32[256,128]{1,0:T(8,128)S(1)}, f32[256,128]{1,0:T(8,128)S(1)}, u32[]{:S(2)}, u32[]{:S(2)}) collective-permute-start(f32[256,128]{1,0:T(8,128)S(1)} %bitcast.4), channel_id=1, source_target_pairs={{0,24},{8,16},{16,8},{24,0},{1,25},{9,17},{17,9},{25,1},{2,26},{10... | collective-permute-start | bytes 393224 | tf_op jit(solution)/shard_map/ppermute | solution.py:816
  66.8 6.5 %collective-permute-start.9 = (f32[256,128]{1,0:T(8,128)S(1)}, f32[256,128]{1,0:T(8,128)S(1)}, u32[]{:S(2)}, u32[]{:S(2)}) collective-permute-start(f32[256,128]{1,0:T(8,128)S(1)} %bitcast.5), channel_id=1, source_target_pairs={{0,8},{8,0},{16,24},{24,16},{1,9},{9,1},{17,25},{25,17},{2,10},{10... | collective-permute-start | bytes 393224 | tf_op jit(solution)/shard_map/ppermute | solution.py:816
